TPU v7x, 128 devices: a whole 4x4x4 slice. The times are simulated.
128 devices in a mesh: slab: 128 (over z, x, y, core).
Axes of the slice: x: 4, y: 4, z: 4, core: 2. Of those that a mesh axis runs over, the one named last changes fastest.
Arguments:
- offsets: float32 [2, 128, 16, 128], P(None, 'slab'), may hold values from 0 to 1
- velocity: float32 [2, 128, 16, 128], P(None, 'slab'), may hold values from -4 to 4
- affine: float32 [4, 128, 16, 128], P(None, 'slab'), may hold values from -1.5 to 1.5
- strain: float32 [4, 128, 16, 128], P(None, 'slab'), may hold values from -0.3 to 0.3
- tile_fill: int32 [128, 16], P('slab'), may hold values from 32 to 128
- force_field: float32 [2, 512, 1024], P(None, 'slab'), may hold values from -6 to 6
- cotangent: float32 [12, 128, 16, 128], P(None, 'slab'), may hold values from -6 to 6
Outputs:
- state_grad: float32 [12, 128, 16, 128], P(None, 'slab')
- force_grad: float32 [2, 512, 1024], P(None, 'slab')
All inputs are finite; a program needn't handle non-finite values.
Results may differ from a plain program's by a relative error of at most 0.0003.
Values sent between devices are 32-bit elements; how exact they have to be, the bound alone decides.
A program may use at most 64 MiB of HBM per device.

v0:
```python
import functools

import jax
import jax.numpy as jnp
from jax import lax
from jax.experimental import pallas as pl
from jax.experimental.pallas import tpu as pltpu
from jax.sharding import PartitionSpec as P

BR = 4
BC = 64
NB = 16
NP = 128
STEPS = 4
COLS = 8
DT = 0.1
F32 = jnp.float32
BF16 = jnp.bfloat16
MESH = pl.DeviceIdType.MESH
SHIFTS = (-1, 0, 1)

EXCHANGES = 7
MAX_CH = 5


def row_spline(d):
    m = jnp.abs(d)
    t = jnp.maximum(1.5 - m, 0.0)
    near = m < 0.5
    value = jnp.where(near, 0.75 - m * m, 0.5 * t * t)
    return value, t, near


def row_slope(d, t, near):
    return jnp.where(near, -2.0 * d, jnp.where(d > 0.0, -t, t))


def col_center(p1):
    return jnp.floor(p1 + 0.5)


def col_parts(p1):
    c = col_center(p1)
    d0 = c - p1
    lo, hi = 0.5 + d0, 0.5 - d0
    values = (0.5 * lo * lo, 0.75 - d0 * d0, 0.5 * hi * hi)
    slopes = (lo, -2.0 * d0, -hi)
    w, wp, dc = [], [], []
    for s, value, slope in zip(SHIFTS, values, slopes):
        inside = jnp.logical_and(c >= float(-s), c <= float(2 * BC - 1 - s))
        w.append(jnp.where(inside, value, 0.0))
        wp.append(jnp.where(inside, slope, 0.0))
        dc.append(jnp.where(inside, d0 + float(s), 0.0))
    return c, w, wp, dc


def split_rows(x):
    top = x.astype(BF16).astype(F32)
    return jnp.concatenate([top, x - top], axis=0)


def roll(x, by):
    return pltpu.roll(x, by % x.shape[-1], axis=x.ndim - 1)


def kernel(
    n,
    off,
    vel,
    aff,
    strn,
    fill,
    force,
    cot,
    sg,
    fg,
    st,
    amat,
    alive_ref,
    hot,
    qm,
    ev,
    od,
    part,
    vg,
    inv,
    frc,
    gat,
    tsave,
    adj,
    fgacc,
    send,
    recv,
    send_sem,
    recv_sem,
):
    me = lax.axis_index("slab")
    right, left = lax.rem(me + 1, n), lax.rem(me + n - 1, n)
    barrier = pltpu.get_barrier_semaphore()
    for other in (left, right):
        pl.semaphore_signal(barrier, inc=1, device_id=(other,), device_id_type=MESH)

    lane16 = lax.broadcasted_iota(jnp.int32, (16, 128), 1)
    sub8 = lax.broadcasted_iota(jnp.int32, (8, 128), 0)
    lane8 = lax.broadcasted_iota(jnp.int32, (8, 128), 1)
    rows8 = sub8.astype(F32)
    top_half = sub8 < 4
    left_half = lane8 < 64

    eye = lax.broadcasted_iota(jnp.int32, (16, 16), 0) == lax.broadcasted_iota(jnp.int32, (16, 16), 1)
    fills = jnp.where(eye, jnp.broadcast_to(fill[...].astype(F32), (16, 16)), 0.0)
    count = jnp.sum(fills, axis=1, keepdims=True)
    alive_ref[...] = jnp.where(lane16.astype(F32) < count, 1.0, 0.0)
    st[0, 0] = BR // 2 + BR * off[0]
    st[0, 1] = BC // 2 + BC * off[1]
    for i in range(2):
        st[0, 2 + i] = vel[i]
    for i in range(4):
        st[0, 4 + i] = aff[i]
        st[0, 8 + i] = strn[i] + (1.0 if i in (0, 3) else 0.0)
    for a in range(2):
        rows = DT * force[a]
        zero = jnp.zeros((2, COLS * 128), F32)
        frc[a] = roll(jnp.concatenate([zero, rows, zero], axis=0), BC // 2)

    def prepare_forward(k):
        alive = alive_ref[...]
        p1 = st[k, 1]
        f00, f01, f10, f11 = (st[k, 8 + i] for i in range(4))
        jac = f00 * f11 - f01 * f10
        pressure = 2.0 * (jac - 1.0) * jac
        sxx = 2.0 * (f00 * f00 + f01 * f01 - 1.0) + pressure
        sxy = 2.0 * (f00 * f10 + f01 * f11)
        syy = 2.0 * (f10 * f10 + f11 * f11 - 1.0) + pressure
        tau = (sxx, sxy, sxy, syy)
        a_mat = []
        for i in range(4):
            value = alive * (-0.4 * tau[i] + st[k, 4 + i])
            amat[k, i] = value
            a_mat.append(value)
        c, w, _, dc = col_parts(p1)
        moved = (alive * st[k, 2], alive * st[k, 3])
        for j in range(3):
            wd = w[j] * dc[j]
            qm[j] = w[j] * alive
            for a in range(2):
                qm[3 + 3 * a + j] = w[j] * moved[a] + wd * a_mat[2 * a + 1]
                qm[9 + 3 * a + j] = w[j] * a_mat[2 * a]
        qm[30] = st[k, 0]
        qm[31] = jnp.where(c < 0.0, c + 128.0, jnp.where(c > 127.0, c - 128.0, c))

    def build_hot(k):
        nodes = lax.broadcasted_iota(jnp.int32, (128, 128), 0).astype(F32)
        for b in range(NB):
            row = qm[31, pl.ds(b, 1), :]
            hot[k, b] = jnp.where(nodes == jnp.broadcast_to(row, (128, 128)), 1.0, 0.0).astype(BF16)

    def adjoint_rows(k, base):
        f00, f01, f10, f11 = (st[k, 8 + i] for i in range(4))
        gf = [adj[8 + i] for i in range(4)]
        v = [adj[2 + a] + DT * adj[a] for a in range(2)]
        x = []
        for a in range(2):
            g0, g1 = gf[2 * a], gf[2 * a + 1]
            x.append(4.0 * (adj[4 + 2 * a] + DT * (g0 * f00 + g1 * f01)))
            x.append(4.0 * (adj[5 + 2 * a] + DT * (g0 * f10 + g1 * f11)))
        _, w, _, dc = col_parts(st[k, 1])
        for j in range(3):
            wd = w[j] * dc[j]
            for a in range(2):
                qm[base + 3 * a + j] = w[j] * v[a] + wd * x[2 * a + 1]
                qm[base + 6 + 3 * a + j] = w[j] * x[2 * a]
        qm[30] = st[k, 0]
        return v, x

    def scatter(k, rows):
        for b in range(NB):
            d = rows8 - jnp.broadcast_to(qm[30, pl.ds(b, 1), :], (8, 128))
            nr, _, _ = row_spline(d)
            nd = nr * d
            pieces = []
            for channel in rows:
                for q, m in channel:
                    x = nr * jnp.broadcast_to(qm[q, pl.ds(b, 1), :], (8, 128))
                    if m is not None:
                        x = x + nd * jnp.broadcast_to(qm[m, pl.ds(b, 1), :], (8, 128))
                    pieces.append(split_rows(x))
            lhs = jnp.concatenate(pieces, axis=0).astype(BF16)
            out = lax.dot_general(
                lhs, hot[k, b], (((1,), (1,)), ((), ())), preferred_element_type=F32
            )
            target = ev if b % 2 == 0 else od
            for ch in range(len(rows)):
                total = None
                for j, s in enumerate(SHIFTS):
                    at = (3 * ch + j) * 16
                    value = out[at : at + 8] + out[at + 8 : at + 16]
                    if s:
                        value = roll(value, s)
                    total = value if total is None else total + value
                if b % 2:
                    total = roll(total, 64)
                target[ch, b // 2] = total

    def forward_channels():
        return [[(j, None) for j in range(3)]] + [
            [(3 + 3 * a + j, 9 + 3 * a + j) for j in range(3)] for a in range(2)
        ]

    def adjoint_channels(base):
        return [[(base + 3 * a + j, base + 6 + 3 * a + j) for j in range(3)] for a in range(2)]

    def pack_and_send(e, count, with_force):
        for ch in range(count):
            sums = []
            for i in range(COLS):
                value = ev[ch, i] + jnp.where(left_half, od[ch, (i - 1) % COLS], od[ch, i])
                if with_force and ch in (1, 2):
                    value = value + frc[ch - 1, :, pl.ds(i * 128, 128)]
                part[ch, :, pl.ds(i * 128, 128)] = value
                sums.append(value)
            for i in range(COLS // 2):
                a, b = sums[2 * i], sums[2 * i + 1]
                down = jnp.where(top_half, pltpu.roll(a, 4, axis=0), b)
                up = jnp.where(top_half, a, pltpu.roll(b, 4, axis=0))
                send[e, 0, ch, :, pl.ds(i * 128, 128)] = down
                send[e, 1, ch, :, pl.ds(i * 128, 128)] = up
        for copy in copies(e, count):
            copy.start()

    def copies(e, count):
        return [
            pltpu.make_async_remote_copy(
                src_ref=send.at[e, side, pl.ds(0, count)],
                dst_ref=recv.at[e, side, pl.ds(0, count)],
                send_sem=send_sem.at[e, side],
                recv_sem=recv_sem.at[e, side],
                device_id=(other,),
                device_id_type=MESH,
            )
            for side, other in ((0, right), (1, left))
        ]

    def summed(e, ch, i):
        above = recv[e, 0, ch, :, pl.ds(i * 128, 128)]
        below = recv[e, 1, ch, :, pl.ds(i * 128, 128)]
        first = jnp.where(top_half, above, pltpu.roll(below, 4, axis=0))
        second = jnp.where(top_half, pltpu.roll(above, 4, axis=0), below)
        return (
            part[ch, :, pl.ds(2 * i * 128, 128)] + first,
            part[ch, :, pl.ds((2 * i + 1) * 128, 128)] + second,
        )

    def wait_halo(e, count):
        for copy in copies(e, count):
            copy.wait_recv()

    def grid_velocity(k, e):
        for i in range(COLS // 2):
            mass = summed(e, 0, i)
            mom = [summed(e, 1 + a, i) for a in range(2)]
            for h in range(2):
                at = pl.ds((2 * i + h) * 128, 128)
                inverse = 1.0 / (mass[h] + 0.25)
                inv[k, :, at] = inverse
                for a in range(2):
                    vg[k, a, :, at] = mom[a][h] * inverse

    def grid_adjoint(k, e, base):
        for i in range(COLS // 2):
            u = [summed(e, base + a, i) for a in range(2)]
            for h in range(2):
                at = pl.ds((2 * i + h) * 128, 128)
                inverse = inv[k, :, at]
                total = u[0][h] * vg[k, 0, :, at] + u[1][h] * vg[k, 1, :, at]
                part[0, :, at] = -total * inverse
                for a in range(2):
                    value = u[a][h] * inverse
                    part[1 + a, :, at] = value
                    fgacc[a, :, at] = fgacc[a, :, at] + DT * value

    def gather(k, column, channels):
        stride = 3 * channels * 64
        for b in range(NB):
            i = b // 2
            pieces = []
            for ch in range(channels):
                window = column(ch, i)
                if b % 2:
                    window = roll(jnp.where(left_half, column(ch, (i + 1) % COLS), window), 64)
                for s in SHIFTS:
                    pieces.append(split_rows(roll(window, -s) if s else window))
            lhs = jnp.concatenate(pieces, axis=0).astype(BF16)
            out = jnp.dot(lhs, hot[k, b], preferred_element_type=F32)
            for q in range(3 * channels):
                value = out[16 * q : 16 * q + 8] + out[16 * q + 8 : 16 * q + 16]
                gat[pl.ds((b // 8) * stride + q * 64 + b % 8, 8, stride=8), :] = value

    def gathered(half, channels, q, r):
        return gat[pl.ds(half * 3 * channels * 64 + q * 64 + r * 8, 8), :]

    def row_sums(half, channels, q, weights):
        totals = [None] * len(weights)
        for r in range(2 * BR):
            g = gathered(half, channels, q, r)
            for t, weight in enumerate(weights):
                value = weight[r] * g
                totals[t] = value if totals[t] is None else totals[t] + value
        return totals

    def dot3(a, b):
        return a[0] * b[0] + a[1] * b[1] + a[2] * b[2]

    def row_weights(p0, slopes):
        plain, slant, slope, slope_d = [], [], [], []
        for r in range(2 * BR):
            d = float(r) - p0
            value, t, near = row_spline(d)
            plain.append(value)
            slant.append(value * d)
            if slopes:
                der = row_slope(d, t, near)
                slope.append(der)
                slope_d.append(der * d)
        return (plain, slant, slope, slope_d) if slopes else (plain, slant)

    def advance(k, store_state):
        for half in range(2):
            at = pl.ds(8 * half, 8)
            p0, p1 = st[k, 0, at], st[k, 1, at]
            weights = row_weights(p0, False)
            _, w, _, dc = col_parts(p1)
            wd = [w[j] * dc[j] for j in range(3)]
            new_v, new_c = [], []
            for a in range(2):
                sums = [row_sums(half, 2, 3 * a + j, weights) for j in range(3)]
                r0 = [x[0] for x in sums]
                r1 = [x[1] for x in sums]
                new_v.append(dot3(w, r0))
                new_c.append(4.0 * dot3(w, r1))
                new_c.append(4.0 * dot3(wd, r0))
            for a in range(2):
                tsave[k, a, at] = new_v[a]
            for i in range(4):
                tsave[k, 2 + i, at] = new_c[i]
            if store_state:
                f = [st[k, 8 + i, at] for i in range(4)]
                st[k + 1, 0, at] = p0 + DT * new_v[0]
                st[k + 1, 1, at] = p1 + DT * new_v[1]
                for a in range(2):
                    st[k + 1, 2 + a, at] = new_v[a]
                for i in range(4):
                    st[k + 1, 4 + i, at] = new_c[i]
                for a in range(2):
                    c0, c1 = DT * new_c[2 * a], DT * new_c[2 * a + 1]
                    for j in range(2):
                        st[k + 1, 8 + 2 * a + j, at] = f[2 * a + j] + (c0 * f[j] + c1 * f[2 + j])

    def slopes_of(half, channels, first, p0, p1, count, plain_only):
        weights = row_weights(p0, True)
        _, w, wp, dc = col_parts(p1)
        wd = [w[j] * dc[j] for j in range(3)]
        wpd = [wp[j] * dc[j] for j in range(3)]
        results = []
        for ch in range(first, first + count):
            if ch < plain_only:
                sums = [row_sums(half, channels, 3 * ch + j, (weights[0], weights[2])) for j in range(3)]
                r0, r2 = ([x[t] for x in sums] for t in range(2))
                results.append((dot3(w, r2), dot3(wp, r0)))
                continue
            sums = [row_sums(half, channels, 3 * ch + j, weights) for j in range(3)]
            r0, r1, r2, r3 = ([x[t] for x in sums] for t in range(4))
            results.append(
                dict(
                    nw=dot3(w, r0),
                    dw=dot3(w, r1),
                    nwd=dot3(wd, r0),
                    pw=dot3(w, r2),
                    pdw=dot3(w, r3),
                    pwd=dot3(wd, r2),
                    nwp=dot3(wp, r0),
                    dwp=dot3(wp, r1),
                    nwpd=dot3(wpd, r0),
                )
            )
        return results

    def save_slopes(k):
        for half in range(2):
            at = pl.ds(8 * half, 8)
            found = slopes_of(half, 2, 0, st[k, 0, at], st[k, 1, at], 2, 0)
            for a, t in enumerate(found):
                for i, name in enumerate(("pw", "pdw", "pwd", "nwp", "dwp", "nwpd")):
                    value = t[name]
                    if name in ("pdw", "nwpd"):
                        value = value + t["nw"]
                    tsave[k, 6 + 6 * a + i, at] = value

    def pull_gather(k, v, x):
        gf = [adj[8 + i] for i in range(4)]
        p0, p1 = adj[0], adj[1]
        for a in range(2):
            pw, pdw, pwd, nwp, dwp, nwpd = (tsave[k, 6 + 6 * a + i] for i in range(6))
            p0 = p0 - (v[a] * pw + x[2 * a] * pdw + x[2 * a + 1] * pwd)
            p1 = p1 - (v[a] * nwp + x[2 * a] * dwp + x[2 * a + 1] * nwpd)
        adj[0] = p0
        adj[1] = p1
        c = [tsave[k, 2 + i] for i in range(4)]
        for b in range(2):
            for j in range(2):
                adj[8 + 2 * b + j] = gf[2 * b + j] + DT * (c[b] * gf[j] + c[2 + b] * gf[2 + j])

    def pull_scatter(k):
        for half in range(2):
            at = pl.ds(8 * half, 8)
            alive = alive_ref[at]
            p0, p1 = st[k, 0, at], st[k, 1, at]
            mass, px, py = slopes_of(half, 3, 0, p0, p1, 3, 1)
            a_mat = [amat[k, i, at] for i in range(4)]
            g0 = adj[0, at] - alive * mass[0]
            g1 = adj[1, at] - alive * mass[1]
            back = []
            for a, t in enumerate((px, py)):
                moved = alive * st[k, 2 + a, at]
                a0, a1 = a_mat[2 * a], a_mat[2 * a + 1]
                g0 = g0 - (moved * t["pw"] + a0 * (t["pdw"] + t["nw"]) + a1 * t["pwd"])
                g1 = g1 - (moved * t["nwp"] + a0 * t["dwp"] + a1 * (t["nwpd"] + t["nw"]))
                adj[2 + a, at] = alive * t["nw"]
                back += [alive * t["dw"], alive * t["nwd"]]
            adj[0, at] = g0
            adj[1, at] = g1
            for i in range(4):
                adj[4 + i, at] = back[i]
            f00, f01, f10, f11 = (st[k, 8 + i, at] for i in range(4))
            sxx, syy = -0.4 * back[0], -0.4 * back[3]
            sxy = -0.4 * (back[1] + back[2])
            jac = f00 * f11 - f01 * f10
            gj = (sxx + syy) * (2.0 * (2.0 * jac - 1.0))
            adj[8, at] = adj[8, at] + (4.0 * f00 * sxx + 2.0 * f10 * sxy + gj * f11)
            adj[9, at] = adj[9, at] + (4.0 * f01 * sxx + 2.0 * f11 * sxy - gj * f10)
            adj[10, at] = adj[10, at] + (4.0 * f10 * syy + 2.0 * f00 * sxy - gj * f01)
            adj[11, at] = adj[11, at] + (4.0 * f11 * syy + 2.0 * f01 * sxy + gj * f00)

    def grid_column(k):
        return lambda ch, i: vg[k, ch, :, pl.ds(i * 128, 128)]

    def part_column(ch, i):
        return part[ch, :, pl.ds(i * 128, 128)]

    def forward_step(k, first):
        prepare_forward(k)
        build_hot(k)
        scatter(k, forward_channels())
        if first:
            pl.semaphore_wait(barrier, 2)
        pack_and_send(k, 3, True)
        if not first:
            save_slopes(k - 1)
        wait_halo(k, 3)
        grid_velocity(k, k)
        gather(k, grid_column(k), 2)
        advance(k, True)

    forward_step(0, True)

    def forward_body(k, carry):
        forward_step(k, False)
        return carry

    lax.fori_loop(1, STEPS - 1, forward_body, 0)

    last = STEPS - 1
    for i in range(12):
        adj[i] = cot[i] * alive_ref[...]
    for a in range(2):
        fgacc[a] = jnp.zeros((8, COLS * 128), F32)
    prepare_forward(last)
    build_hot(last)
    adjoint_rows(last, 15)
    scatter(last, forward_channels() + adjoint_channels(15))
    pack_and_send(last, 5, True)
    save_slopes(last - 1)
    wait_halo(last, 5)
    grid_velocity(last, last)
    gather(last, grid_column(last), 2)
    advance(last, False)
    save_slopes(last)
    v, x = adjoint_rows(last, 15)
    pull_gather(last, v, x)
    grid_adjoint(last, last, 3)
    gather(last, part_column, 3)
    pull_scatter(last)

    def backward_body(t, carry):
        k = last - 1 - t
        e = last + 1 + t
        v, x = adjoint_rows(k, 15)
        scatter(k, adjoint_channels(15))
        pack_and_send(e, 2, False)
        pull_gather(k, v, x)
        wait_halo(e, 2)
        grid_adjoint(k, e, 0)
        gather(k, part_column, 3)
        pull_scatter(k)
        return carry

    lax.fori_loop(0, STEPS - 1, backward_body, 0)

    sg[0] = adj[0] * float(BR)
    sg[1] = adj[1] * float(BC)
    for i in range(2, 12):
        sg[i] = adj[i]
    for a in range(2):
        fg[a] = roll(fgacc[a], -(BC // 2))[2:6]
    for e in range(EXCHANGES):
        for copy in copies(e, 3 if e < last else (5 if e == last else 2)):
            copy.wait_send()


def per_device(n, offsets, velocity, affine, strain, tile_fill, force_field, cotangent):
    def flat(x):
        return x.reshape(x.shape[0], NB, NP)

    vmem = pl.BlockSpec(memory_space=pltpu.VMEM)
    width = COLS * 128
    state_grad, force_grad = pl.pallas_call(
        functools.partial(kernel, n),
        out_shape=(
            jax.ShapeDtypeStruct((12, NB, NP), F32),
            jax.ShapeDtypeStruct((2, BR, width), F32),
        ),
        in_specs=[vmem] * 7,
        out_specs=(vmem, vmem),
        scratch_shapes=[
            pltpu.VMEM((STEPS, 12, NB, NP), F32),
            pltpu.VMEM((STEPS, 4, NB, NP), F32),
            pltpu.VMEM((NB, NP), F32),
            pltpu.VMEM((STEPS, NB, 128, NP), BF16),
            pltpu.VMEM((32, NB, NP), F32),
            pltpu.VMEM((MAX_CH, COLS, 8, 128), F32),
            pltpu.VMEM((MAX_CH, COLS, 8, 128), F32),
            pltpu.VMEM((MAX_CH, 8, width), F32),
            pltpu.VMEM((STEPS, 2, 8, width), F32),
            pltpu.VMEM((STEPS, 8, width), F32),
            pltpu.VMEM((2, 8, width), F32),
            pltpu.VMEM((2 * 72 * 8, 128), F32),
            pltpu.VMEM((STEPS, 18, NB, NP), F32),
            pltpu.VMEM((12, NB, NP), F32),
            pltpu.VMEM((2, 8, width), F32),
            pltpu.VMEM((EXCHANGES, 2, MAX_CH, 8, width // 2), F32),
            pltpu.VMEM((EXCHANGES, 2, MAX_CH, 8, width // 2), F32),
            pltpu.SemaphoreType.DMA((EXCHANGES, 2)),
            pltpu.SemaphoreType.DMA((EXCHANGES, 2)),
        ],
        compiler_params=pltpu.CompilerParams(collective_id=0, has_side_effects=True),
    )(
        flat(offsets),
        flat(velocity),
        flat(affine),
        flat(strain),
        tile_fill,
        force_field,
        flat(cotangent),
    )
    return state_grad.reshape(12, 1, NB, NP), force_grad


def solution(mesh):
    n = mesh.shape["slab"]
    tiles = P(None, "slab", None, None)
    return jax.shard_map(
        functools.partial(per_device, n),
        mesh=mesh,
        in_specs=(tiles, tiles, tiles, tiles, P("slab", None), P(None, "slab", None), tiles),
        out_specs=(tiles, P(None, "slab", None)),
        check_vma=False,
    )
```

profile of v0, /device:TPU:0, one launch (start us, length us, event | category | flops | bytes accessed | tf_op | source)
XLA Modules:
  0.0 57.1 jit_solution(1106162850749160997)
XLA Ops:
  0.6 54.2 %shard_map.86 = (f32[12,16,128]{2,1,0:T(8,128)}, f32[2,4,1024]{2,1,0:T(4,128)}) custom-call(f32[2,16,128]{2,1,0:T(8,128)} %bitcast.12, f32[2,16,128]{2,1,0:T(8,128)} %bitcast.13, f32[4,16,128]{2,1,0:T(8,128)} %bitcast.10, f32[4,16,128]{2,1,0:T(8,128)} %bitcast.11, s32[1,16]{1,0:T(1,128)} %fill.1, f32[2,4,1024]{2,1,0:T(4,128)} %force.1, f32[12,16,128]{2,1,0:T(8,128)} %bitcast.8), custom_call_target="tpu_custom_call" | custom-call | tf_op jit(solution)/shard_map/pallas_call | solution.py:526
  54.9 0.0 copy-start
  54.9 1.5 %copy.12 = f32[12,1,16,128]{3,2,1,0:T(8,128)} copy(f32[12,1,16,128]{3,2,1,0:T(8,128)} %bitcast.9) | data formatting | bytes 196608
  56.4 0.0 copy-done
  56.4 0.6 %copy.13 = f32[2,4,1024]{2,1,0:T(4,128)} copy(f32[2,4,1024]{2,1,0:T(4,128)S(1)} %copy-done) | data formatting | bytes 65536
Async XLA Ops:
  54.9 1.6 %copy-start = (f32[2,4,1024]{2,1,0:T(4,128)S(1)}, f32[2,4,1024]{2,1,0:T(4,128)}, u32[]{:S(2)}) copy-start(f32[2,4,1024]{2,1,0:T(4,128)} %get-tuple-element.11) | copy-start | bytes 98308
where the time goes:
time: 57.2 us; the launch traced here: 57.1 us
  Pallas kernels  54.2 us (95%)
  local copies, waits for them, and re-layouts  2.16 us (4%)
  between operations  0.65 us (1%)
    pallas_call x1, Pallas kernels, per_device(): pl.pallas_call(functools.partial(kernel, n), out_shape=(jax.ShapeDtypeStr...  54.2 us
    unnamed x4, local copies, waits for them, and re-layouts  2.16 us

commit v1 on v0

--- a/solution.py
+++ b/solution.py
@@ -19,8 +19,29 @@
 MESH = pl.DeviceIdType.MESH
 SHIFTS = (-1, 0, 1)
 
-EXCHANGES = 7
+EXCHANGES = 8
 MAX_CH = 5
+OWN = STEPS
+RAW, COT, FORCE, ADJ, FGRAD = range(5)
+CHIPS = {64: (4, 4, 4), 8: (2, 2, 2), 4: (1, 2, 2)}
+
+
+def host_of(band, n):
+    _, nx, ny = CHIPS[n // 2]
+    core, chip = lax.rem(band, 2), lax.div(band, 2)
+    y, x, z = lax.rem(chip, ny), lax.rem(lax.div(chip, ny), nx), lax.div(chip, nx * ny)
+    y = y + lax.rem(x, 2) * (ny - 1 - 2 * y)
+    x = x + lax.rem(z, 2) * (nx - 1 - 2 * x)
+    return ((z * nx + x) * ny + y) * 2 + core
+
+
+def band_of(device, n):
+    _, nx, ny = CHIPS[n // 2]
+    core, chip = lax.rem(device, 2), lax.div(device, 2)
+    y, x, z = lax.rem(chip, ny), lax.rem(lax.div(chip, ny), nx), lax.div(chip, nx * ny)
+    x = x + lax.rem(z, 2) * (nx - 1 - 2 * x)
+    y = y + lax.rem(x, 2) * (ny - 1 - 2 * y)
+    return ((z * nx + x) * ny + y) * 2 + core
 
 
 def row_spline(d):
@@ -65,40 +86,125 @@
 
 def kernel(
     n,
-    off,
-    vel,
-    aff,
-    strn,
+    off_hbm,
+    vel_hbm,
+    aff_hbm,
+    strn_hbm,
+    fill_hbm,
+    force_hbm,
+    cot_hbm,
+    sg,
+    fg,
     fill,
+    raw,
     force,
     cot,
-    sg,
-    fg,
     st,
     amat,
-    alive_ref,
     hot,
     qm,
     ev,
     od,
-    part,
+    parts,
     vg,
     inv,
     frc,
     gat,
     tsave,
-    adj,
+    adjs,
     fgacc,
+    fgmove,
     send,
     recv,
+    load_sem,
     send_sem,
     recv_sem,
+    move_send,
+    move_recv,
 ):
     me = lax.axis_index("slab")
-    right, left = lax.rem(me + 1, n), lax.rem(me + n - 1, n)
+    band = band_of(me, n)
+    home = host_of(me, n)
+    moved = home != me
+    stays = home == me
+
+    def after(i):
+        return lax.rem(i + 1, n)
+
+    def before(i):
+        return lax.rem(i + n - 1, n)
+
+    ring = (host_of(after(band), n), host_of(before(band), n))
+    to_hosts = (host_of(after(me), n), host_of(before(me), n))
+    to_owners = (after(band), before(band))
+    owners = (after(me), before(me))
+
+    loads = [
+        pltpu.make_async_copy(src, dst, load_sem.at[i])
+        for i, (src, dst) in enumerate(
+            (
+                (off_hbm, raw.at[1, pl.ds(0, 2)]),
+                (vel_hbm, raw.at[1, pl.ds(2, 2)]),
+                (aff_hbm, raw.at[1, pl.ds(4, 4)]),
+                (strn_hbm, raw.at[1, pl.ds(8, 4)]),
+                (fill_hbm, fill),
+                (force_hbm, force.at[1]),
+                (cot_hbm, cot.at[1]),
+            )
+        )
+    ]
+    for load in loads:
+        load.start()
+
     barrier = pltpu.get_barrier_semaphore()
-    for other in (left, right):
+    for other in ring + to_hosts + to_owners + owners:
         pl.semaphore_signal(barrier, inc=1, device_id=(other,), device_id_type=MESH)
+
+    @pl.when(moved)
+    def _():
+        pl.semaphore_signal(barrier, inc=1, device_id=(home,), device_id_type=MESH)
+        pl.semaphore_signal(barrier, inc=1, device_id=(band,), device_id_type=MESH)
+
+    def barrier_wait():
+        @pl.when(moved)
+        def _():
+            pl.semaphore_wait(barrier, 10)
+
+        @pl.when(stays)
+        def _():
+            pl.semaphore_wait(barrier, 8)
+
+    def move(which, src, dst, device):
+        return pltpu.make_async_remote_copy(
+            src_ref=src,
+            dst_ref=dst,
+            send_sem=move_send.at[which],
+            recv_sem=move_recv.at[which],
+            device_id=(device,),
+            device_id_type=MESH,
+        )
+
+    moves = [
+        move(RAW, raw.at[1], raw.at[0], home),
+        move(COT, cot.at[1], cot.at[0], home),
+        move(FORCE, force.at[1], force.at[0], home),
+        move(ADJ, adjs.at[0], adjs.at[1], band),
+        move(FGRAD, fgmove.at[0], fgmove.at[1], band),
+    ]
+
+    def start_move(which):
+        @pl.when(moved)
+        def _():
+            moves[which].start()
+
+    def end_move(which, ref, src, dst):
+        @pl.when(moved)
+        def _():
+            moves[which].wait_recv()
+
+        @pl.when(stays)
+        def _():
+            ref[dst] = ref[src]
 
     lane16 = lax.broadcasted_iota(jnp.int32, (16, 128), 1)
     sub8 = lax.broadcasted_iota(jnp.int32, (8, 128), 0)
@@ -107,24 +213,27 @@
     top_half = sub8 < 4
     left_half = lane8 < 64
 
+    def initial_state(role, k):
+        st[k, 0] = BR // 2 + BR * raw[role, 0]
+        st[k, 1] = BC // 2 + BC * raw[role, 1]
+        for i in range(2, 12):
+            st[k, i] = raw[role, i] + (1.0 if i in (8, 11) else 0.0)
+
+    def place_force(role):
+        for a in range(2):
+            rows = DT * force[role, a]
+            zero = jnp.zeros((2, COLS * 128), F32)
+            frc[role, a] = roll(jnp.concatenate([zero, rows, zero], axis=0), BC // 2)
+
+    for i in (4, 0, 1, 2, 3):
+        loads[i].wait()
     eye = lax.broadcasted_iota(jnp.int32, (16, 16), 0) == lax.broadcasted_iota(jnp.int32, (16, 16), 1)
     fills = jnp.where(eye, jnp.broadcast_to(fill[...].astype(F32), (16, 16)), 0.0)
     count = jnp.sum(fills, axis=1, keepdims=True)
-    alive_ref[...] = jnp.where(lane16.astype(F32) < count, 1.0, 0.0)
-    st[0, 0] = BR // 2 + BR * off[0]
-    st[0, 1] = BC // 2 + BC * off[1]
-    for i in range(2):
-        st[0, 2 + i] = vel[i]
-    for i in range(4):
-        st[0, 4 + i] = aff[i]
-        st[0, 8 + i] = strn[i] + (1.0 if i in (0, 3) else 0.0)
-    for a in range(2):
-        rows = DT * force[a]
-        zero = jnp.zeros((2, COLS * 128), F32)
-        frc[a] = roll(jnp.concatenate([zero, rows, zero], axis=0), BC // 2)
-
-    def prepare_forward(k):
-        alive = alive_ref[...]
+    raw[1, 12] = jnp.where(lane16.astype(F32) < count, 1.0, 0.0)
+
+    def prepare_forward(k, role):
+        alive = raw[role, 12]
         p1 = st[k, 1]
         f00, f01, f10, f11 = (st[k, 8 + i] for i in range(4))
         jac = f00 * f11 - f01 * f10
@@ -155,7 +264,7 @@
             row = qm[31, pl.ds(b, 1), :]
             hot[k, b] = jnp.where(nodes == jnp.broadcast_to(row, (128, 128)), 1.0, 0.0).astype(BF16)
 
-    def adjoint_rows(k, base):
+    def adjoint_rows(k, base, adj):
         f00, f01, f10, f11 = (st[k, 8 + i] for i in range(4))
         gf = [adj[8 + i] for i in range(4)]
         v = [adj[2 + a] + DT * adj[a] for a in range(2)]
@@ -210,38 +319,42 @@
     def adjoint_channels(base):
         return [[(base + 3 * a + j, base + 6 + 3 * a + j) for j in range(3)] for a in range(2)]
 
-    def pack_and_send(e, count, with_force):
+    def combine(count, part, force_role):
         for ch in range(count):
-            sums = []
             for i in range(COLS):
                 value = ev[ch, i] + jnp.where(left_half, od[ch, (i - 1) % COLS], od[ch, i])
-                if with_force and ch in (1, 2):
-                    value = value + frc[ch - 1, :, pl.ds(i * 128, 128)]
+                if force_role is not None and ch in (1, 2):
+                    value = value + frc[force_role, ch - 1, :, pl.ds(i * 128, 128)]
                 part[ch, :, pl.ds(i * 128, 128)] = value
-                sums.append(value)
+
+    def pack(e, count, part):
+        for ch in range(count):
             for i in range(COLS // 2):
-                a, b = sums[2 * i], sums[2 * i + 1]
+                a = part[ch, :, pl.ds(2 * i * 128, 128)]
+                b = part[ch, :, pl.ds((2 * i + 1) * 128, 128)]
                 down = jnp.where(top_half, pltpu.roll(a, 4, axis=0), b)
                 up = jnp.where(top_half, a, pltpu.roll(b, 4, axis=0))
                 send[e, 0, ch, :, pl.ds(i * 128, 128)] = down
                 send[e, 1, ch, :, pl.ds(i * 128, 128)] = up
-        for copy in copies(e, count):
-            copy.start()
-
-    def copies(e, count):
+
+    def copies(e, count, targets, source=None):
         return [
             pltpu.make_async_remote_copy(
-                src_ref=send.at[e, side, pl.ds(0, count)],
+                src_ref=send.at[e if source is None else source, side, pl.ds(0, count)],
                 dst_ref=recv.at[e, side, pl.ds(0, count)],
                 send_sem=send_sem.at[e, side],
                 recv_sem=recv_sem.at[e, side],
                 device_id=(other,),
                 device_id_type=MESH,
             )
-            for side, other in ((0, right), (1, left))
+            for side, other in enumerate(targets)
         ]
 
-    def summed(e, ch, i):
+    def start_halo(e, count, targets, source=None):
+        for copy in copies(e, count, targets, source):
+            copy.start()
+
+    def summed(e, part, ch, i):
         above = recv[e, 0, ch, :, pl.ds(i * 128, 128)]
         below = recv[e, 1, ch, :, pl.ds(i * 128, 128)]
         first = jnp.where(top_half, above, pltpu.roll(below, 4, axis=0))
@@ -251,14 +364,14 @@
             part[ch, :, pl.ds((2 * i + 1) * 128, 128)] + second,
         )
 
-    def wait_halo(e, count):
-        for copy in copies(e, count):
+    def wait_halo(e, count, targets, source=None):
+        for copy in copies(e, count, targets, source):
             copy.wait_recv()
 
-    def grid_velocity(k, e):
+    def grid_velocity(k, e, part):
         for i in range(COLS // 2):
-            mass = summed(e, 0, i)
-            mom = [summed(e, 1 + a, i) for a in range(2)]
+            mass = summed(e, part, 0, i)
+            mom = [summed(e, part, 1 + a, i) for a in range(2)]
             for h in range(2):
                 at = pl.ds((2 * i + h) * 128, 128)
                 inverse = 1.0 / (mass[h] + 0.25)
@@ -266,9 +379,9 @@
                 for a in range(2):
                     vg[k, a, :, at] = mom[a][h] * inverse
 
-    def grid_adjoint(k, e, base):
+    def grid_adjoint(k, e, base, part, first):
         for i in range(COLS // 2):
-            u = [summed(e, base + a, i) for a in range(2)]
+            u = [summed(e, part, base + a, i) for a in range(2)]
             for h in range(2):
                 at = pl.ds((2 * i + h) * 128, 128)
                 inverse = inv[k, :, at]
@@ -277,7 +390,7 @@
                 for a in range(2):
                     value = u[a][h] * inverse
                     part[1 + a, :, at] = value
-                    fgacc[a, :, at] = fgacc[a, :, at] + DT * value
+                    fgacc[a, :, at] = DT * value if first else fgacc[a, :, at] + DT * value
 
     def gather(k, column, channels):
         stride = 3 * channels * 64
@@ -396,7 +509,7 @@
                         value = value + t["nw"]
                     tsave[k, 6 + 6 * a + i, at] = value
 
-    def pull_gather(k, v, x):
+    def pull_gather(k, v, x, adj):
         gf = [adj[8 + i] for i in range(4)]
         p0, p1 = adj[0], adj[1]
         for a in range(2):
@@ -410,10 +523,10 @@
             for j in range(2):
                 adj[8 + 2 * b + j] = gf[2 * b + j] + DT * (c[b] * gf[j] + c[2 + b] * gf[2 + j])
 
-    def pull_scatter(k):
+    def pull_scatter(k, role, adj):
         for half in range(2):
             at = pl.ds(8 * half, 8)
-            alive = alive_ref[at]
+            alive = raw[role, 12, at]
             p0, p1 = st[k, 0, at], st[k, 1, at]
             mass, px, py = slopes_of(half, 3, 0, p0, p1, 3, 1)
             a_mat = [amat[k, i, at] for i in range(4)]
@@ -444,76 +557,133 @@
     def grid_column(k):
         return lambda ch, i: vg[k, ch, :, pl.ds(i * 128, 128)]
 
-    def part_column(ch, i):
-        return part[ch, :, pl.ds(i * 128, 128)]
-
-    def forward_step(k, first):
-        prepare_forward(k)
+    def part_column(part):
+        return lambda ch, i: part[ch, :, pl.ds(i * 128, 128)]
+
+    def forward_front(k, role):
+        prepare_forward(k, role)
         build_hot(k)
         scatter(k, forward_channels())
-        if first:
-            pl.semaphore_wait(barrier, 2)
-        pack_and_send(k, 3, True)
-        if not first:
-            save_slopes(k - 1)
-        wait_halo(k, 3)
-        grid_velocity(k, k)
+
+    def forward_back(k, e, part, store_state):
+        grid_velocity(k, e, part)
         gather(k, grid_column(k), 2)
-        advance(k, True)
-
-    forward_step(0, True)
-
-    def forward_body(k, carry):
-        forward_step(k, False)
-        return carry
-
-    lax.fori_loop(1, STEPS - 1, forward_body, 0)
-
+        advance(k, store_state)
+
+    part, part_own = parts.at[0], parts.at[1]
+    adj, adj_own = adjs.at[0], adjs.at[1]
     last = STEPS - 1
+
+    initial_state(1, OWN)
+    forward_front(OWN, 1)
+    loads[5].wait()
+    loads[6].wait()
+    place_force(1)
+    combine(3, part_own, 1)
+    barrier_wait()
+    start_move(RAW)
+    pack(0, 3, part_own)
+    start_halo(0, 3, to_hosts)
+    start_move(FORCE)
+    start_move(COT)
+    start_halo(7, 3, owners, 0)
+
+    end_move(RAW, raw, 1, 0)
+    initial_state(0, 0)
+    forward_front(0, 0)
+    end_move(FORCE, force, 1, 0)
+    place_force(0)
+    combine(3, part, 0)
+    wait_halo(0, 3, to_hosts)
+    forward_back(0, 0, part, True)
+
+    for k in range(1, last):
+        forward_front(k, 0)
+        combine(3, part, 0)
+        pack(k, 3, part)
+        start_halo(k, 3, ring)
+        save_slopes(k - 1)
+        if k == 1:
+            wait_halo(7, 3, owners, 0)
+            forward_back(OWN, 7, part_own, False)
+            save_slopes(OWN)
+        wait_halo(k, 3, ring)
+        forward_back(k, k, part, True)
+
+    end_move(COT, cot, 1, 0)
     for i in range(12):
-        adj[i] = cot[i] * alive_ref[...]
-    for a in range(2):
-        fgacc[a] = jnp.zeros((8, COLS * 128), F32)
-    prepare_forward(last)
+        adj[i] = cot[0, i] * raw[0, 12]
+    adjoint_rows(last, 15, adj)
+    prepare_forward(last, 0)
     build_hot(last)
-    adjoint_rows(last, 15)
     scatter(last, forward_channels() + adjoint_channels(15))
-    pack_and_send(last, 5, True)
+    combine(5, part, 0)
+    pack(last, 5, part)
+    start_halo(last, 5, ring)
     save_slopes(last - 1)
-    wait_halo(last, 5)
-    grid_velocity(last, last)
-    gather(last, grid_column(last), 2)
-    advance(last, False)
+    wait_halo(last, 5, ring)
+    forward_back(last, last, part, False)
     save_slopes(last)
-    v, x = adjoint_rows(last, 15)
-    pull_gather(last, v, x)
-    grid_adjoint(last, last, 3)
-    gather(last, part_column, 3)
-    pull_scatter(last)
+    v, x = adjoint_rows(last, 15, adj)
+    pull_gather(last, v, x, adj)
+    grid_adjoint(last, last, 3, part, True)
+    gather(last, part_column(part), 3)
+    pull_scatter(last, 0, adj)
 
     def backward_body(t, carry):
         k = last - 1 - t
         e = last + 1 + t
-        v, x = adjoint_rows(k, 15)
+        v, x = adjoint_rows(k, 15, adj)
         scatter(k, adjoint_channels(15))
-        pack_and_send(e, 2, False)
-        pull_gather(k, v, x)
-        wait_halo(e, 2)
-        grid_adjoint(k, e, 0)
-        gather(k, part_column, 3)
-        pull_scatter(k)
+        combine(2, part, None)
+        pack(e, 2, part)
+        start_halo(e, 2, ring)
+        pull_gather(k, v, x, adj)
+        wait_halo(e, 2, ring)
+        grid_adjoint(k, e, 0, part, False)
+        gather(k, part_column(part), 3)
+        pull_scatter(k, 0, adj)
         return carry
 
-    lax.fori_loop(0, STEPS - 1, backward_body, 0)
-
-    sg[0] = adj[0] * float(BR)
-    sg[1] = adj[1] * float(BC)
+    lax.fori_loop(0, STEPS - 2, backward_body, 0)
+
+    adjoint_rows(0, 15, adj)
+    start_move(ADJ)
+    scatter(0, adjoint_channels(15))
+    combine(2, part, None)
+    pack(6, 2, part)
+    start_halo(6, 2, to_owners)
+    for a in range(2):
+        fgmove[0, a] = roll(fgacc[a], -(BC // 2))[2:6]
+    start_move(FGRAD)
+
+    end_move(ADJ, adjs, 0, 1)
+    v, x = adjoint_rows(OWN, 15, adj_own)
+    scatter(OWN, adjoint_channels(15))
+    combine(2, part_own, None)
+    pull_gather(OWN, v, x, adj_own)
+    wait_halo(6, 2, to_owners)
+    grid_adjoint(OWN, 6, 0, part_own, True)
+    gather(OWN, part_column(part_own), 3)
+    pull_scatter(OWN, 1, adj_own)
+
+    sg[0] = adj_own[0] * float(BR)
+    sg[1] = adj_own[1] * float(BC)
     for i in range(2, 12):
-        sg[i] = adj[i]
+        sg[i] = adj_own[i]
+    end_move(FGRAD, fgmove, 0, 1)
     for a in range(2):
-        fg[a] = roll(fgacc[a], -(BC // 2))[2:6]
+        fg[a] = fgmove[1, a] + roll(fgacc[a], -(BC // 2))[2:6]
+
     for e in range(EXCHANGES):
-        for copy in copies(e, 3 if e < last else (5 if e == last else 2)):
+        targets = {0: to_hosts, 6: to_owners, 7: owners}.get(e, ring)
+        count = 5 if e == last else (2 if e in (4, 5, 6) else 3)
+        for copy in copies(e, count, targets, 0 if e == 7 else None):
+            copy.wait_send()
+
+    @pl.when(moved)
+    def _():
+        for copy in moves:
             copy.wait_send()
 
 
@@ -529,28 +699,35 @@
             jax.ShapeDtypeStruct((12, NB, NP), F32),
             jax.ShapeDtypeStruct((2, BR, width), F32),
         ),
-        in_specs=[vmem] * 7,
+        in_specs=[pl.BlockSpec(memory_space=pl.ANY)] * 7,
         out_specs=(vmem, vmem),
         scratch_shapes=[
-            pltpu.VMEM((STEPS, 12, NB, NP), F32),
-            pltpu.VMEM((STEPS, 4, NB, NP), F32),
-            pltpu.VMEM((NB, NP), F32),
-            pltpu.VMEM((STEPS, NB, 128, NP), BF16),
+            pltpu.VMEM((1, NB), jnp.int32),
+            pltpu.VMEM((2, 13, NB, NP), F32),
+            pltpu.VMEM((2, 2, BR, width), F32),
+            pltpu.VMEM((2, 12, NB, NP), F32),
+            pltpu.VMEM((STEPS + 1, 12, NB, NP), F32),
+            pltpu.VMEM((STEPS + 1, 4, NB, NP), F32),
+            pltpu.VMEM((STEPS + 1, NB, 128, NP), BF16),
             pltpu.VMEM((32, NB, NP), F32),
             pltpu.VMEM((MAX_CH, COLS, 8, 128), F32),
             pltpu.VMEM((MAX_CH, COLS, 8, 128), F32),
-            pltpu.VMEM((MAX_CH, 8, width), F32),
-            pltpu.VMEM((STEPS, 2, 8, width), F32),
-            pltpu.VMEM((STEPS, 8, width), F32),
+            pltpu.VMEM((2, MAX_CH, 8, width), F32),
+            pltpu.VMEM((STEPS + 1, 2, 8, width), F32),
+            pltpu.VMEM((STEPS + 1, 8, width), F32),
+            pltpu.VMEM((2, 2, 8, width), F32),
+            pltpu.VMEM((2 * 72 * 8, 128), F32),
+            pltpu.VMEM((STEPS + 1, 18, NB, NP), F32),
+            pltpu.VMEM((2, 12, NB, NP), F32),
             pltpu.VMEM((2, 8, width), F32),
-            pltpu.VMEM((2 * 72 * 8, 128), F32),
-            pltpu.VMEM((STEPS, 18, NB, NP), F32),
-            pltpu.VMEM((12, NB, NP), F32),
-            pltpu.VMEM((2, 8, width), F32),
+            pltpu.VMEM((2, 2, BR, width), F32),
             pltpu.VMEM((EXCHANGES, 2, MAX_CH, 8, width // 2), F32),
             pltpu.VMEM((EXCHANGES, 2, MAX_CH, 8, width // 2), F32),
+            pltpu.SemaphoreType.DMA((7,)),
             pltpu.SemaphoreType.DMA((EXCHANGES, 2)),
             pltpu.SemaphoreType.DMA((EXCHANGES, 2)),
+            pltpu.SemaphoreType.DMA((5,)),
+            pltpu.SemaphoreType.DMA((5,)),
         ],
         compiler_params=pltpu.CompilerParams(collective_id=0, has_side_effects=True),
     )(

time: 57.2 us -> 48.1 us (0.84)
  Pallas kernels: 54.2 us -> 45.1 us
    pallas_call x1, Pallas kernels: 54.2 us -> 45.1 us  [per_device(): pl.pallas_call(functools.partial(kernel, n), out_shape=(jax.ShapeDtypeStr...]
where the time goes in v1:
time: 48.1 us; the launch traced here: 47.9 us
  Pallas kernels  45.1 us (94%)
  local copies, waits for them, and re-layouts  2.16 us (4%)
  between operations  0.65 us (1%)
    pallas_call x1, Pallas kernels, per_device(): pl.pallas_call(functools.partial(kernel, n), out_shape=(jax.ShapeDtypeStr...  45.1 us
    unnamed x4, local copies, waits for them, and re-layouts  2.16 us

profile of v1, /device:TPU:0, one launch (start us, length us, event | category | flops | bytes accessed | tf_op | source)
XLA Modules:
  0.0 47.9 jit_solution(13219775950355824415)
XLA Ops:
  0.6 45.1 %shard_map.86 = (f32[12,16,128]{2,1,0:T(8,128)}, f32[2,4,1024]{2,1,0:T(4,128)}) custom-call(f32[2,16,128]{2,1,0:T(8,128)} %bitcast.12, f32[2,16,128]{2,1,0:T(8,128)} %bitcast.13, f32[4,16,128]{2,1,0:T(8,128)} %bitcast.10, f32[4,16,128]{2,1,0:T(8,128)} %bitcast.11, s32[1,16]{1,0:T(1,128)} %fill_hbm.1, f32[2,4,1024]{2,1,0:T(4,128)} %force_hbm.1, ...), custom_call_target="tpu_custom_call" | custom-call | tf_op jit(solution)/shard_map/pallas_call | solution.py:696
  45.7 0.0 copy-start
  45.8 1.5 %copy.12 = f32[12,1,16,128]{3,2,1,0:T(8,128)} copy(f32[12,1,16,128]{3,2,1,0:T(8,128)} %bitcast.9) | data formatting | bytes 196608
  47.3 0.0 copy-done
  47.3 0.6 %copy.13 = f32[2,4,1024]{2,1,0:T(4,128)} copy(f32[2,4,1024]{2,1,0:T(4,128)S(1)} %copy-done) | data formatting | bytes 65536
Async XLA Ops:
  45.7 1.6 %copy-start = (f32[2,4,1024]{2,1,0:T(4,128)S(1)}, f32[2,4,1024]{2,1,0:T(4,128)}, u32[]{:S(2)}) copy-start(f32[2,4,1024]{2,1,0:T(4,128)} %get-tuple-element.11) | copy-start | bytes 98308

commit v2 on v1

--- a/solution.py
+++ b/solution.py
@@ -22,7 +22,7 @@
 EXCHANGES = 8
 MAX_CH = 5
 OWN = STEPS
-RAW, COT, FORCE, ADJ, FGRAD = range(5)
+RAW, STRAIN, COT, FORCE, RATES, ADJ, FGRAD = range(7)
 CHIPS = {64: (4, 4, 4), 8: (2, 2, 2), 4: (1, 2, 2)}
 
 
@@ -97,6 +97,11 @@
     fg,
     fill,
     raw,
+    aff,
+    strn,
+    first,
+    rates,
+    rest,
     force,
     cot,
     st,
@@ -143,10 +148,10 @@
         pltpu.make_async_copy(src, dst, load_sem.at[i])
         for i, (src, dst) in enumerate(
             (
-                (off_hbm, raw.at[1, pl.ds(0, 2)]),
-                (vel_hbm, raw.at[1, pl.ds(2, 2)]),
-                (aff_hbm, raw.at[1, pl.ds(4, 4)]),
-                (strn_hbm, raw.at[1, pl.ds(8, 4)]),
+                (off_hbm, raw.at[pl.ds(0, 2)]),
+                (vel_hbm, raw.at[pl.ds(2, 2)]),
+                (aff_hbm, aff),
+                (strn_hbm, strn.at[1]),
                 (fill_hbm, fill),
                 (force_hbm, force.at[1]),
                 (cot_hbm, cot.at[1]),
@@ -185,10 +190,12 @@
         )
 
     moves = [
-        move(RAW, raw.at[1], raw.at[0], home),
+        move(RAW, first.at[1], first.at[0], home),
+        move(STRAIN, strn.at[1], strn.at[0], home),
         move(COT, cot.at[1], cot.at[0], home),
         move(FORCE, force.at[1], force.at[0], home),
-        move(ADJ, adjs.at[0], adjs.at[1], band),
+        move(RATES, rates.at[0], rates.at[1], band),
+        move(ADJ, rest.at[0], rest.at[1], band),
         move(FGRAD, fgmove.at[0], fgmove.at[1], band),
     ]
 
@@ -213,11 +220,20 @@
     top_half = sub8 < 4
     left_half = lane8 < 64
 
-    def initial_state(role, k):
-        st[k, 0] = BR // 2 + BR * raw[role, 0]
-        st[k, 1] = BC // 2 + BC * raw[role, 1]
-        for i in range(2, 12):
-            st[k, i] = raw[role, i] + (1.0 if i in (8, 11) else 0.0)
+    def load_state():
+        for i, value in enumerate(
+            (BR // 2 + BR * raw[0], BC // 2 + BC * raw[1], raw[2], raw[3])
+        ):
+            st[OWN, i] = value
+            first[1, i] = value
+        for i in range(4):
+            st[OWN, 4 + i] = aff[i]
+            st[OWN, 8 + i] = strn[1, i] + (1.0 if i in (0, 3) else 0.0)
+
+    def host_state():
+        for i in range(4):
+            st[0, i] = first[0, i]
+            amat[0, i] = first[0, 5 + i]
 
     def place_force(role):
         for a in range(2):
@@ -230,11 +246,10 @@
     eye = lax.broadcasted_iota(jnp.int32, (16, 16), 0) == lax.broadcasted_iota(jnp.int32, (16, 16), 1)
     fills = jnp.where(eye, jnp.broadcast_to(fill[...].astype(F32), (16, 16)), 0.0)
     count = jnp.sum(fills, axis=1, keepdims=True)
-    raw[1, 12] = jnp.where(lane16.astype(F32) < count, 1.0, 0.0)
-
-    def prepare_forward(k, role):
-        alive = raw[role, 12]
-        p1 = st[k, 1]
+    first[1, 4] = jnp.where(lane16.astype(F32) < count, 1.0, 0.0)
+
+    def stress_matrix(k, role):
+        alive = first[role, 4]
         f00, f01, f10, f11 = (st[k, 8 + i] for i in range(4))
         jac = f00 * f11 - f01 * f10
         pressure = 2.0 * (jac - 1.0) * jac
@@ -242,11 +257,16 @@
         sxy = 2.0 * (f00 * f10 + f01 * f11)
         syy = 2.0 * (f10 * f10 + f11 * f11 - 1.0) + pressure
         tau = (sxx, sxy, sxy, syy)
-        a_mat = []
         for i in range(4):
             value = alive * (-0.4 * tau[i] + st[k, 4 + i])
             amat[k, i] = value
-            a_mat.append(value)
+            if k is OWN:
+                first[1, 5 + i] = value
+
+    def prepare_forward(k, role):
+        alive = first[role, 4]
+        p1 = st[k, 1]
+        a_mat = [amat[k, i] for i in range(4)]
         c, w, _, dc = col_parts(p1)
         moved = (alive * st[k, 2], alive * st[k, 3])
         for j in range(3):
@@ -281,6 +301,17 @@
                 qm[base + 6 + 3 * a + j] = w[j] * x[2 * a]
         qm[30] = st[k, 0]
         return v, x
+
+    def rate_rows(k):
+        v = [rates[1, a] for a in range(2)]
+        x = [rates[1, 2 + i] for i in range(4)]
+        _, w, _, dc = col_parts(st[k, 1])
+        for j in range(3):
+            wd = w[j] * dc[j]
+            for a in range(2):
+                qm[15 + 3 * a + j] = w[j] * v[a] + wd * x[2 * a + 1]
+                qm[21 + 3 * a + j] = w[j] * x[2 * a]
+        qm[30] = st[k, 0]
 
     def scatter(k, rows):
         for b in range(NB):
@@ -526,7 +557,7 @@
     def pull_scatter(k, role, adj):
         for half in range(2):
             at = pl.ds(8 * half, 8)
-            alive = raw[role, 12, at]
+            alive = first[role, 4, at]
             p0, p1 = st[k, 0, at], st[k, 1, at]
             mass, px, py = slopes_of(half, 3, 0, p0, p1, 3, 1)
             a_mat = [amat[k, i, at] for i in range(4)]
@@ -561,6 +592,8 @@
         return lambda ch, i: part[ch, :, pl.ds(i * 128, 128)]
 
     def forward_front(k, role):
+        if k or role:
+            stress_matrix(k, role)
         prepare_forward(k, role)
         build_hot(k)
         scatter(k, forward_channels())
@@ -574,7 +607,7 @@
     adj, adj_own = adjs.at[0], adjs.at[1]
     last = STEPS - 1
 
-    initial_state(1, OWN)
+    load_state()
     forward_front(OWN, 1)
     loads[5].wait()
     loads[6].wait()
@@ -585,16 +618,20 @@
     pack(0, 3, part_own)
     start_halo(0, 3, to_hosts)
     start_move(FORCE)
+    start_move(STRAIN)
     start_move(COT)
     start_halo(7, 3, owners, 0)
 
-    end_move(RAW, raw, 1, 0)
-    initial_state(0, 0)
+    end_move(RAW, first, 1, 0)
+    host_state()
     forward_front(0, 0)
     end_move(FORCE, force, 1, 0)
     place_force(0)
     combine(3, part, 0)
     wait_halo(0, 3, to_hosts)
+    end_move(STRAIN, strn, 1, 0)
+    for i in range(4):
+        st[0, 8 + i] = strn[0, i] + (1.0 if i in (0, 3) else 0.0)
     forward_back(0, 0, part, True)
 
     for k in range(1, last):
@@ -605,15 +642,15 @@
         save_slopes(k - 1)
         if k == 1:
             wait_halo(7, 3, owners, 0)
-            forward_back(OWN, 7, part_own, False)
-            save_slopes(OWN)
+            grid_velocity(OWN, 7, part_own)
         wait_halo(k, 3, ring)
         forward_back(k, k, part, True)
 
     end_move(COT, cot, 1, 0)
     for i in range(12):
-        adj[i] = cot[0, i] * raw[0, 12]
+        adj[i] = cot[0, i] * first[0, 4]
     adjoint_rows(last, 15, adj)
+    stress_matrix(last, 0)
     prepare_forward(last, 0)
     build_hot(last)
     scatter(last, forward_channels() + adjoint_channels(15))
@@ -647,24 +684,32 @@
 
     lax.fori_loop(0, STEPS - 2, backward_body, 0)
 
-    adjoint_rows(0, 15, adj)
-    start_move(ADJ)
+    v, x = adjoint_rows(0, 15, adj)
+    for i, value in enumerate(v + x):
+        rates[0, i] = value
     scatter(0, adjoint_channels(15))
+    start_move(RATES)
     combine(2, part, None)
     pack(6, 2, part)
     start_halo(6, 2, to_owners)
+    pull_gather(0, v, x, adj)
+    for i in range(6):
+        rest[0, i] = adj[i if i < 2 else 6 + i]
     for a in range(2):
         fgmove[0, a] = roll(fgacc[a], -(BC // 2))[2:6]
+    start_move(ADJ)
     start_move(FGRAD)
 
-    end_move(ADJ, adjs, 0, 1)
-    v, x = adjoint_rows(OWN, 15, adj_own)
+    end_move(RATES, rates, 0, 1)
+    rate_rows(OWN)
     scatter(OWN, adjoint_channels(15))
     combine(2, part_own, None)
-    pull_gather(OWN, v, x, adj_own)
     wait_halo(6, 2, to_owners)
     grid_adjoint(OWN, 6, 0, part_own, True)
     gather(OWN, part_column(part_own), 3)
+    end_move(ADJ, rest, 0, 1)
+    for i in range(6):
+        adj_own[i if i < 2 else 6 + i] = rest[1, i]
     pull_scatter(OWN, 1, adj_own)
 
     sg[0] = adj_own[0] * float(BR)
@@ -699,11 +744,16 @@
             jax.ShapeDtypeStruct((12, NB, NP), F32),
             jax.ShapeDtypeStruct((2, BR, width), F32),
         ),
-        in_specs=[pl.BlockSpec(memory_space=pl.ANY)] * 7,
+        in_specs=[pl.BlockSpec(memory_space=pltpu.HBM)] * 7,
         out_specs=(vmem, vmem),
         scratch_shapes=[
             pltpu.VMEM((1, NB), jnp.int32),
-            pltpu.VMEM((2, 13, NB, NP), F32),
+            pltpu.VMEM((4, NB, NP), F32),
+            pltpu.VMEM((4, NB, NP), F32),
+            pltpu.VMEM((2, 4, NB, NP), F32),
+            pltpu.VMEM((2, 9, NB, NP), F32),
+            pltpu.VMEM((2, 6, NB, NP), F32),
+            pltpu.VMEM((2, 6, NB, NP), F32),
             pltpu.VMEM((2, 2, BR, width), F32),
             pltpu.VMEM((2, 12, NB, NP), F32),
             pltpu.VMEM((STEPS + 1, 12, NB, NP), F32),
@@ -726,8 +776,8 @@
             pltpu.SemaphoreType.DMA((7,)),
             pltpu.SemaphoreType.DMA((EXCHANGES, 2)),
             pltpu.SemaphoreType.DMA((EXCHANGES, 2)),
-            pltpu.SemaphoreType.DMA((5,)),
-            pltpu.SemaphoreType.DMA((5,)),
+            pltpu.SemaphoreType.DMA((7,)),
+            pltpu.SemaphoreType.DMA((7,)),
         ],
         compiler_params=pltpu.CompilerParams(collective_id=0, has_side_effects=True),
     )(

time: 48.1 us -> 47.6 us (0.990)
  Pallas kernels: 45.1 us -> 44.5 us
    pallas_call x1, Pallas kernels: 45.1 us -> 44.5 us  [per_device(): pl.pallas_call(functools.partial(kernel, n), out_shape=(jax.ShapeDtypeStr...]
where the time goes in v2:
time: 47.6 us; the launch traced here: 47.4 us
  Pallas kernels  44.5 us (93%)
  local copies, waits for them, and re-layouts  2.16 us (5%)
  between operations  0.65 us (1%)
    pallas_call x1, Pallas kernels, per_device(): pl.pallas_call(functools.partial(kernel, n), out_shape=(jax.ShapeDtypeStr...  44.5 us
    unnamed x4, local copies, waits for them, and re-layouts  2.16 us

profile of v2, /device:TPU:0, one launch (start us, length us, event | category | flops | bytes accessed | tf_op | source)
XLA Modules:
  0.0 47.4 jit_solution(6167355718581128972)
XLA Ops:
  0.6 44.5 %shard_map.86 = (f32[12,16,128]{2,1,0:T(8,128)}, f32[2,4,1024]{2,1,0:T(4,128)}) custom-call(f32[2,16,128]{2,1,0:T(8,128)} %bitcast.12, f32[2,16,128]{2,1,0:T(8,128)} %bitcast.13, f32[4,16,128]{2,1,0:T(8,128)} %bitcast.10, f32[4,16,128]{2,1,0:T(8,128)} %bitcast.11, s32[1,16]{1,0:T(1,128)} %fill_hbm.1, f32[2,4,1024]{2,1,0:T(4,128)} %force_hbm.1, ...), custom_call_target="tpu_custom_call" | custom-call | tf_op jit(solution)/shard_map/pallas_call | solution.py:741
  45.2 0.0 copy-start
  45.2 1.5 %copy.12 = f32[12,1,16,128]{3,2,1,0:T(8,128)} copy(f32[12,1,16,128]{3,2,1,0:T(8,128)} %bitcast.9) | data formatting | bytes 196608
  46.7 0.0 copy-done
  46.7 0.6 %copy.13 = f32[2,4,1024]{2,1,0:T(4,128)} copy(f32[2,4,1024]{2,1,0:T(4,128)S(1)} %copy-done) | data formatting | bytes 65536
Async XLA Ops:
  45.2 1.6 %copy-start = (f32[2,4,1024]{2,1,0:T(4,128)S(1)}, f32[2,4,1024]{2,1,0:T(4,128)}, u32[]{:S(2)}) copy-start(f32[2,4,1024]{2,1,0:T(4,128)} %get-tuple-element.11) | copy-start | bytes 98308

commit v3 on v2

--- a/solution.py
+++ b/solution.py
@@ -21,6 +21,10 @@
 
 EXCHANGES = 8
 MAX_CH = 5
+CHUNKS = 2
+SCATTER_BLOCKS = ((15, 0, 1, 2, 3, 4, 5, 6, 7), (8, 9, 10, 11, 12, 13, 14))
+GATHER_BLOCKS = ((0, 1, 2, 3, 4, 5, 6), (7, 8, 9, 10, 11, 12, 13, 14, 15))
+CHUNK_COLS = ((0, 1, 2, 3), (4, 5, 6, 7))
 OWN = STEPS
 RAW, STRAIN, COT, FORCE, RATES, ADJ, FGRAD = range(7)
 CHIPS = {64: (4, 4, 4), 8: (2, 2, 2), 4: (1, 2, 2)}
@@ -313,8 +317,8 @@
                 qm[21 + 3 * a + j] = w[j] * x[2 * a]
         qm[30] = st[k, 0]
 
-    def scatter(k, rows):
-        for b in range(NB):
+    def scatter(k, rows, blocks=range(NB)):
+        for b in blocks:
             d = rows8 - jnp.broadcast_to(qm[30, pl.ds(b, 1), :], (8, 128))
             nr, _, _ = row_spline(d)
             nd = nr * d
@@ -350,82 +354,93 @@
     def adjoint_channels(base):
         return [[(base + 3 * a + j, base + 6 + 3 * a + j) for j in range(3)] for a in range(2)]
 
-    def combine(count, part, force_role):
+    def combine(count, part, force_role, cols=range(COLS)):
         for ch in range(count):
-            for i in range(COLS):
+            for i in cols:
                 value = ev[ch, i] + jnp.where(left_half, od[ch, (i - 1) % COLS], od[ch, i])
                 if force_role is not None and ch in (1, 2):
                     value = value + frc[force_role, ch - 1, :, pl.ds(i * 128, 128)]
                 part[ch, :, pl.ds(i * 128, 128)] = value
 
-    def pack(e, count, part):
+    def pack(e, c, count, part):
         for ch in range(count):
-            for i in range(COLS // 2):
-                a = part[ch, :, pl.ds(2 * i * 128, 128)]
-                b = part[ch, :, pl.ds((2 * i + 1) * 128, 128)]
+            for i in range(2):
+                at = CHUNK_COLS[c][2 * i] * 128
+                a = part[ch, :, pl.ds(at, 128)]
+                b = part[ch, :, pl.ds(at + 128, 128)]
                 down = jnp.where(top_half, pltpu.roll(a, 4, axis=0), b)
                 up = jnp.where(top_half, a, pltpu.roll(b, 4, axis=0))
-                send[e, 0, ch, :, pl.ds(i * 128, 128)] = down
-                send[e, 1, ch, :, pl.ds(i * 128, 128)] = up
-
-    def copies(e, count, targets, source=None):
+                send[e, c, 0, ch, :, pl.ds(i * 128, 128)] = down
+                send[e, c, 1, ch, :, pl.ds(i * 128, 128)] = up
+
+    def copies(e, c, count, targets, source=None):
         return [
             pltpu.make_async_remote_copy(
-                src_ref=send.at[e if source is None else source, side, pl.ds(0, count)],
-                dst_ref=recv.at[e, side, pl.ds(0, count)],
-                send_sem=send_sem.at[e, side],
-                recv_sem=recv_sem.at[e, side],
+                src_ref=send.at[e if source is None else source, c, side, pl.ds(0, count)],
+                dst_ref=recv.at[e, c, side, pl.ds(0, count)],
+                send_sem=send_sem.at[e, c, side],
+                recv_sem=recv_sem.at[e, c, side],
                 device_id=(other,),
                 device_id_type=MESH,
             )
             for side, other in enumerate(targets)
         ]
 
-    def start_halo(e, count, targets, source=None):
-        for copy in copies(e, count, targets, source):
+    def start_halo(e, c, count, targets, source=None):
+        for copy in copies(e, c, count, targets, source):
             copy.start()
 
-    def summed(e, part, ch, i):
-        above = recv[e, 0, ch, :, pl.ds(i * 128, 128)]
-        below = recv[e, 1, ch, :, pl.ds(i * 128, 128)]
+    def wait_halo(e, c, count, targets, source=None):
+        for copy in copies(e, c, count, targets, source):
+            copy.wait_recv()
+
+    def scatter_and_send(e, k, rows, part, force_role, targets, before_first=None):
+        for c in range(CHUNKS):
+            scatter(k, rows, SCATTER_BLOCKS[c])
+            combine(len(rows), part, force_role, CHUNK_COLS[c])
+            pack(e, c, len(rows), part)
+            if before_first is not None and c == 0:
+                before_first()
+            start_halo(e, c, len(rows), targets)
+
+    def summed(e, c, part, ch, i):
+        above = recv[e, c, 0, ch, :, pl.ds(i * 128, 128)]
+        below = recv[e, c, 1, ch, :, pl.ds(i * 128, 128)]
         first = jnp.where(top_half, above, pltpu.roll(below, 4, axis=0))
         second = jnp.where(top_half, pltpu.roll(above, 4, axis=0), below)
+        at = CHUNK_COLS[c][2 * i] * 128
         return (
-            part[ch, :, pl.ds(2 * i * 128, 128)] + first,
-            part[ch, :, pl.ds((2 * i + 1) * 128, 128)] + second,
+            part[ch, :, pl.ds(at, 128)] + first,
+            part[ch, :, pl.ds(at + 128, 128)] + second,
         )
 
-    def wait_halo(e, count, targets, source=None):
-        for copy in copies(e, count, targets, source):
-            copy.wait_recv()
-
-    def grid_velocity(k, e, part):
-        for i in range(COLS // 2):
-            mass = summed(e, part, 0, i)
-            mom = [summed(e, part, 1 + a, i) for a in range(2)]
+    def grid_velocity(k, e, c, part):
+        for i in range(2):
+            mass = summed(e, c, part, 0, i)
+            mom = [summed(e, c, part, 1 + a, i) for a in range(2)]
             for h in range(2):
-                at = pl.ds((2 * i + h) * 128, 128)
+                at = pl.ds(CHUNK_COLS[c][2 * i + h] * 128, 128)
                 inverse = 1.0 / (mass[h] + 0.25)
                 inv[k, :, at] = inverse
                 for a in range(2):
                     vg[k, a, :, at] = mom[a][h] * inverse
 
-    def grid_adjoint(k, e, base, part, first):
-        for i in range(COLS // 2):
-            u = [summed(e, part, base + a, i) for a in range(2)]
+    def grid_adjoint(k, e, c, base, part, initial):
+        for i in range(2):
+            u = [summed(e, c, part, base + a, i) for a in range(2)]
             for h in range(2):
-                at = pl.ds((2 * i + h) * 128, 128)
+                at = pl.ds(CHUNK_COLS[c][2 * i + h] * 128, 128)
                 inverse = inv[k, :, at]
                 total = u[0][h] * vg[k, 0, :, at] + u[1][h] * vg[k, 1, :, at]
                 part[0, :, at] = -total * inverse
                 for a in range(2):
                     value = u[a][h] * inverse
                     part[1 + a, :, at] = value
-                    fgacc[a, :, at] = DT * value if first else fgacc[a, :, at] + DT * value
-
-    def gather(k, column, channels):
+                    fgacc[a, :, at] = DT * value if initial else fgacc[a, :, at] + DT * value
+
+    def gather(k, column, channels, blocks):
         stride = 3 * channels * 64
-        for b in range(NB):
+        for b in blocks:
             i = b // 2
             pieces = []
             for ch in range(channels):
@@ -468,7 +483,7 @@
                 slope_d.append(der * d)
         return (plain, slant, slope, slope_d) if slopes else (plain, slant)
 
-    def advance(k, store_state):
+    def advance(k, store_state, channels=2):
         for half in range(2):
             at = pl.ds(8 * half, 8)
             p0, p1 = st[k, 0, at], st[k, 1, at]
@@ -477,7 +492,7 @@
             wd = [w[j] * dc[j] for j in range(3)]
             new_v, new_c = [], []
             for a in range(2):
-                sums = [row_sums(half, 2, 3 * a + j, weights) for j in range(3)]
+                sums = [row_sums(half, channels, 3 * a + j, weights) for j in range(3)]
                 r0 = [x[0] for x in sums]
                 r1 = [x[1] for x in sums]
                 new_v.append(dot3(w, r0))
@@ -507,7 +522,7 @@
         wpd = [wp[j] * dc[j] for j in range(3)]
         results = []
         for ch in range(first, first + count):
-            if ch < plain_only:
+            if ch < first + plain_only:
                 sums = [row_sums(half, channels, 3 * ch + j, (weights[0], weights[2])) for j in range(3)]
                 r0, r2 = ([x[t] for x in sums] for t in range(2))
                 results.append((dot3(w, r2), dot3(wp, r0)))
@@ -529,10 +544,10 @@
             )
         return results
 
-    def save_slopes(k):
+    def save_slopes(k, channels=2):
         for half in range(2):
             at = pl.ds(8 * half, 8)
-            found = slopes_of(half, 2, 0, st[k, 0, at], st[k, 1, at], 2, 0)
+            found = slopes_of(half, channels, 0, st[k, 0, at], st[k, 1, at], 2, 0)
             for a, t in enumerate(found):
                 for i, name in enumerate(("pw", "pdw", "pwd", "nwp", "dwp", "nwpd")):
                     value = t[name]
@@ -554,12 +569,12 @@
             for j in range(2):
                 adj[8 + 2 * b + j] = gf[2 * b + j] + DT * (c[b] * gf[j] + c[2 + b] * gf[2 + j])
 
-    def pull_scatter(k, role, adj):
+    def pull_scatter(k, role, adj, channels=3):
         for half in range(2):
             at = pl.ds(8 * half, 8)
             alive = first[role, 4, at]
             p0, p1 = st[k, 0, at], st[k, 1, at]
-            mass, px, py = slopes_of(half, 3, 0, p0, p1, 3, 1)
+            mass, px, py = slopes_of(half, channels, channels - 3, p0, p1, 3, 1)
             a_mat = [amat[k, i, at] for i in range(4)]
             g0 = adj[0, at] - alive * mass[0]
             g1 = adj[1, at] - alive * mass[1]
@@ -596,12 +611,19 @@
             stress_matrix(k, role)
         prepare_forward(k, role)
         build_hot(k)
-        scatter(k, forward_channels())
-
-    def forward_back(k, e, part, store_state):
-        grid_velocity(k, e, part)
-        gather(k, grid_column(k), 2)
-        advance(k, store_state)
+
+    def forward_back(k, e, part, targets):
+        for c in range(CHUNKS):
+            wait_halo(e, c, 3, targets)
+            grid_velocity(k, e, c, part)
+            gather(k, grid_column(k), 2, GATHER_BLOCKS[c])
+        advance(k, True)
+
+    def backward_back(k, e, part, initial, targets):
+        for c in range(CHUNKS):
+            wait_halo(e, c, 2, targets)
+            grid_adjoint(k, e, c, 0, part, initial)
+            gather(k, part_column(part), 3, GATHER_BLOCKS[c])
 
     part, part_own = parts.at[0], parts.at[1]
     adj, adj_own = adjs.at[0], adjs.at[1]
@@ -612,39 +634,39 @@
     loads[5].wait()
     loads[6].wait()
     place_force(1)
-    combine(3, part_own, 1)
-    barrier_wait()
-    start_move(RAW)
-    pack(0, 3, part_own)
-    start_halo(0, 3, to_hosts)
+
+    def enter():
+        barrier_wait()
+        start_move(RAW)
+
+    scatter_and_send(0, OWN, forward_channels(), part_own, 1, to_hosts, enter)
     start_move(FORCE)
     start_move(STRAIN)
     start_move(COT)
-    start_halo(7, 3, owners, 0)
+    for c in range(CHUNKS):
+        start_halo(7, c, 3, owners, 0)
 
     end_move(RAW, first, 1, 0)
     host_state()
     forward_front(0, 0)
+    scatter(0, forward_channels())
     end_move(FORCE, force, 1, 0)
     place_force(0)
     combine(3, part, 0)
-    wait_halo(0, 3, to_hosts)
     end_move(STRAIN, strn, 1, 0)
     for i in range(4):
         st[0, 8 + i] = strn[0, i] + (1.0 if i in (0, 3) else 0.0)
-    forward_back(0, 0, part, True)
+    forward_back(0, 0, part, to_hosts)
 
     for k in range(1, last):
         forward_front(k, 0)
-        combine(3, part, 0)
-        pack(k, 3, part)
-        start_halo(k, 3, ring)
+        scatter_and_send(k, k, forward_channels(), part, 0, ring)
         save_slopes(k - 1)
         if k == 1:
-            wait_halo(7, 3, owners, 0)
-            grid_velocity(OWN, 7, part_own)
-        wait_halo(k, 3, ring)
-        forward_back(k, k, part, True)
+            for c in range(CHUNKS):
+                wait_halo(7, c, 3, owners, 0)
+                grid_velocity(OWN, 7, c, part_own)
+        forward_back(k, k, part, ring)
 
     end_move(COT, cot, 1, 0)
     for i in range(12):
@@ -653,32 +675,30 @@
     stress_matrix(last, 0)
     prepare_forward(last, 0)
     build_hot(last)
-    scatter(last, forward_channels() + adjoint_channels(15))
-    combine(5, part, 0)
-    pack(last, 5, part)
-    start_halo(last, 5, ring)
+    scatter_and_send(last, last, forward_channels() + adjoint_channels(15), part, 0, ring)
     save_slopes(last - 1)
-    wait_halo(last, 5, ring)
-    forward_back(last, last, part, False)
-    save_slopes(last)
+
+    def last_column(ch, i):
+        return grid_column(last)(ch, i) if ch < 2 else part_column(part)(ch - 2, i)
+
+    for c in range(CHUNKS):
+        wait_halo(last, c, 5, ring)
+        grid_velocity(last, last, c, part)
+        grid_adjoint(last, last, c, 3, part, True)
+        gather(last, last_column, 5, GATHER_BLOCKS[c])
+    advance(last, False, 5)
+    save_slopes(last, 5)
     v, x = adjoint_rows(last, 15, adj)
     pull_gather(last, v, x, adj)
-    grid_adjoint(last, last, 3, part, True)
-    gather(last, part_column(part), 3)
-    pull_scatter(last, 0, adj)
+    pull_scatter(last, 0, adj, 5)
 
     def backward_body(t, carry):
         k = last - 1 - t
         e = last + 1 + t
         v, x = adjoint_rows(k, 15, adj)
-        scatter(k, adjoint_channels(15))
-        combine(2, part, None)
-        pack(e, 2, part)
-        start_halo(e, 2, ring)
+        scatter_and_send(e, k, adjoint_channels(15), part, None, ring)
         pull_gather(k, v, x, adj)
-        wait_halo(e, 2, ring)
-        grid_adjoint(k, e, 0, part, False)
-        gather(k, part_column(part), 3)
+        backward_back(k, e, part, False, ring)
         pull_scatter(k, 0, adj)
         return carry
 
@@ -687,11 +707,7 @@
     v, x = adjoint_rows(0, 15, adj)
     for i, value in enumerate(v + x):
         rates[0, i] = value
-    scatter(0, adjoint_channels(15))
-    start_move(RATES)
-    combine(2, part, None)
-    pack(6, 2, part)
-    start_halo(6, 2, to_owners)
+    scatter_and_send(6, 0, adjoint_channels(15), part, None, to_owners, lambda: start_move(RATES))
     pull_gather(0, v, x, adj)
     for i in range(6):
         rest[0, i] = adj[i if i < 2 else 6 + i]
@@ -704,9 +720,7 @@
     rate_rows(OWN)
     scatter(OWN, adjoint_channels(15))
     combine(2, part_own, None)
-    wait_halo(6, 2, to_owners)
-    grid_adjoint(OWN, 6, 0, part_own, True)
-    gather(OWN, part_column(part_own), 3)
+    backward_back(OWN, 6, part_own, True, to_owners)
     end_move(ADJ, rest, 0, 1)
     for i in range(6):
         adj_own[i if i < 2 else 6 + i] = rest[1, i]
@@ -723,8 +737,9 @@
     for e in range(EXCHANGES):
         targets = {0: to_hosts, 6: to_owners, 7: owners}.get(e, ring)
         count = 5 if e == last else (2 if e in (4, 5, 6) else 3)
-        for copy in copies(e, count, targets, 0 if e == 7 else None):
-            copy.wait_send()
+        for c in range(CHUNKS):
+            for copy in copies(e, c, count, targets, 0 if e == 7 else None):
+                copy.wait_send()
 
     @pl.when(moved)
     def _():
@@ -766,16 +781,16 @@
             pltpu.VMEM((STEPS + 1, 2, 8, width), F32),
             pltpu.VMEM((STEPS + 1, 8, width), F32),
             pltpu.VMEM((2, 2, 8, width), F32),
-            pltpu.VMEM((2 * 72 * 8, 128), F32),
+            pltpu.VMEM((2 * 120 * 8, 128), F32),
             pltpu.VMEM((STEPS + 1, 18, NB, NP), F32),
             pltpu.VMEM((2, 12, NB, NP), F32),
             pltpu.VMEM((2, 8, width), F32),
             pltpu.VMEM((2, 2, BR, width), F32),
-            pltpu.VMEM((EXCHANGES, 2, MAX_CH, 8, width // 2), F32),
-            pltpu.VMEM((EXCHANGES, 2, MAX_CH, 8, width // 2), F32),
+            pltpu.VMEM((EXCHANGES, CHUNKS, 2, MAX_CH, 8, width // 4), F32),
+            pltpu.VMEM((EXCHANGES, CHUNKS, 2, MAX_CH, 8, width // 4), F32),
             pltpu.SemaphoreType.DMA((7,)),
-            pltpu.SemaphoreType.DMA((EXCHANGES, 2)),
-            pltpu.SemaphoreType.DMA((EXCHANGES, 2)),
+            pltpu.SemaphoreType.DMA((EXCHANGES, CHUNKS, 2)),
+            pltpu.SemaphoreType.DMA((EXCHANGES, CHUNKS, 2)),
             pltpu.SemaphoreType.DMA((7,)),
             pltpu.SemaphoreType.DMA((7,)),
         ],

time: 47.6 us -> 47.7 us (level)
  no operation moved by 1% of the time
where the time goes in v3:
time: 47.7 us; the launch traced here: 47.6 us
  Pallas kernels  44.8 us (94%)
  local copies, waits for them, and re-layouts  2.16 us (5%)
  between operations  0.65 us (1%)
    pallas_call x1, Pallas kernels, per_device(): pl.pallas_call(functools.partial(kernel, n), out_shape=(jax.ShapeDtypeStr...  44.8 us
    unnamed x4, local copies, waits for them, and re-layouts  2.16 us

profile of v3, /device:TPU:0, one launch (start us, length us, event | category | flops | bytes accessed | tf_op | source)
XLA Modules:
  0.0 47.6 jit_solution(3758637101293939129)
XLA Ops:
  0.6 44.8 %shard_map.86 = (f32[12,16,128]{2,1,0:T(8,128)}, f32[2,4,1024]{2,1,0:T(4,128)}) custom-call(f32[2,16,128]{2,1,0:T(8,128)} %bitcast.12, f32[2,16,128]{2,1,0:T(8,128)} %bitcast.13, f32[4,16,128]{2,1,0:T(8,128)} %bitcast.10, f32[4,16,128]{2,1,0:T(8,128)} %bitcast.11, s32[1,16]{1,0:T(1,128)} %fill_hbm.1, f32[2,4,1024]{2,1,0:T(4,128)} %force_hbm.1, ...), custom_call_target="tpu_custom_call" | custom-call | tf_op jit(solution)/shard_map/pallas_call | solution.py:756
  45.4 0.0 copy-start
  45.4 1.5 %copy.12 = f32[12,1,16,128]{3,2,1,0:T(8,128)} copy(f32[12,1,16,128]{3,2,1,0:T(8,128)} %bitcast.9) | data formatting | bytes 196608
  47.0 0.0 copy-done
  47.0 0.6 %copy.13 = f32[2,4,1024]{2,1,0:T(4,128)} copy(f32[2,4,1024]{2,1,0:T(4,128)S(1)} %copy-done) | data formatting | bytes 65536
Async XLA Ops:
  45.4 1.6 %copy-start = (f32[2,4,1024]{2,1,0:T(4,128)S(1)}, f32[2,4,1024]{2,1,0:T(4,128)}, u32[]{:S(2)}) copy-start(f32[2,4,1024]{2,1,0:T(4,128)} %get-tuple-element.11) | copy-start | bytes 98308

commit v4 on v3

--- a/solution.py
+++ b/solution.py
@@ -21,10 +21,10 @@
 
 EXCHANGES = 8
 MAX_CH = 5
-CHUNKS = 2
-SCATTER_BLOCKS = ((15, 0, 1, 2, 3, 4, 5, 6, 7), (8, 9, 10, 11, 12, 13, 14))
-GATHER_BLOCKS = ((0, 1, 2, 3, 4, 5, 6), (7, 8, 9, 10, 11, 12, 13, 14, 15))
-CHUNK_COLS = ((0, 1, 2, 3), (4, 5, 6, 7))
+CHUNKS = 1
+SCATTER_BLOCKS = (tuple(range(NB)),)
+GATHER_BLOCKS = (tuple(range(NB)),)
+CHUNK_COLS = (tuple(range(COLS)),)
 OWN = STEPS
 RAW, STRAIN, COT, FORCE, RATES, ADJ, FGRAD = range(7)
 CHIPS = {64: (4, 4, 4), 8: (2, 2, 2), 4: (1, 2, 2)}
@@ -364,7 +364,7 @@
 
     def pack(e, c, count, part):
         for ch in range(count):
-            for i in range(2):
+            for i in range(len(CHUNK_COLS[c]) // 2):
                 at = CHUNK_COLS[c][2 * i] * 128
                 a = part[ch, :, pl.ds(at, 128)]
                 b = part[ch, :, pl.ds(at + 128, 128)]
@@ -415,7 +415,7 @@
         )
 
     def grid_velocity(k, e, c, part):
-        for i in range(2):
+        for i in range(len(CHUNK_COLS[c]) // 2):
             mass = summed(e, c, part, 0, i)
             mom = [summed(e, c, part, 1 + a, i) for a in range(2)]
             for h in range(2):
@@ -426,7 +426,7 @@
                     vg[k, a, :, at] = mom[a][h] * inverse
 
     def grid_adjoint(k, e, c, base, part, initial):
-        for i in range(2):
+        for i in range(len(CHUNK_COLS[c]) // 2):
             u = [summed(e, c, part, base + a, i) for a in range(2)]
             for h in range(2):
                 at = pl.ds(CHUNK_COLS[c][2 * i + h] * 128, 128)
@@ -786,23 +786,23 @@
             pltpu.VMEM((2, 12, NB, NP), F32),
             pltpu.VMEM((2, 8, width), F32),
             pltpu.VMEM((2, 2, BR, width), F32),
-            pltpu.VMEM((EXCHANGES, CHUNKS, 2, MAX_CH, 8, width // 4), F32),
-            pltpu.VMEM((EXCHANGES, CHUNKS, 2, MAX_CH, 8, width // 4), F32),
+            pltpu.VMEM((EXCHANGES, CHUNKS, 2, MAX_CH, 8, width // 2 // CHUNKS), F32),
+            pltpu.VMEM((EXCHANGES, CHUNKS, 2, MAX_CH, 8, width // 2 // CHUNKS), F32),
             pltpu.SemaphoreType.DMA((7,)),
             pltpu.SemaphoreType.DMA((EXCHANGES, CHUNKS, 2)),
             pltpu.SemaphoreType.DMA((EXCHANGES, CHUNKS, 2)),
             pltpu.SemaphoreType.DMA((7,)),
             pltpu.SemaphoreType.DMA((7,)),
         ],
-        compiler_params=pltpu.CompilerParams(collective_id=0, has_side_effects=True),
+        compiler_params=pltpu.CompilerParams(collective_id=0, has_side_effects=True, vmem_limit_bytes=24 << 20),
     )(
-        flat(offsets),
-        flat(velocity),
-        flat(affine),
-        flat(strain),
-        tile_fill,
-        force_field,
-        flat(cotangent),
+        pltpu.with_memory_space_constraint(flat(offsets), pltpu.HBM),
+        pltpu.with_memory_space_constraint(flat(velocity), pltpu.HBM),
+        pltpu.with_memory_space_constraint(flat(affine), pltpu.HBM),
+        pltpu.with_memory_space_constraint(flat(strain), pltpu.HBM),
+        pltpu.with_memory_space_constraint(tile_fill, pltpu.HBM),
+        pltpu.with_memory_space_constraint(force_field, pltpu.HBM),
+        pltpu.with_memory_space_constraint(flat(cotangent), pltpu.HBM),
     )
     return state_grad.reshape(12, 1, NB, NP), force_grad
 

time: 47.7 us -> 46.4 us (0.973)
  local copies, waits for them, and re-layouts: 2.16 us -> 1.26 us
  Pallas kernels: 44.8 us -> 44.1 us
    unnamed x4 -> x2, local copies, waits for them, and re-layouts: 2.16 us -> 1.26 us
    pallas_call x1, Pallas kernels: 44.8 us -> 44.1 us  [per_device(): pl.pallas_call(functools.partial(kernel, n), out_shape=(jax.ShapeDtypeStr...]
where the time goes in v4:
time: 46.4 us; the launch traced here: 46 us
  Pallas kernels  44.1 us (95%)
  local copies, waits for them, and re-layouts  1.26 us (3%)
  between operations  0.64 us (1%)
    pallas_call x1, Pallas kernels, per_device(): pl.pallas_call(functools.partial(kernel, n), out_shape=(jax.ShapeDtypeStr...  44.1 us
    unnamed x2, local copies, waits for them, and re-layouts  1.26 us

profile of v4, /device:TPU:0, one launch (start us, length us, event | category | flops | bytes accessed | tf_op | source)
XLA Modules:
  0.0 46.0 jit_solution(5262719658344315544)
XLA Ops:
  0.6 44.1 %shard_map.86 = (f32[12,16,128]{2,1,0:T(8,128)S(1)}, f32[2,4,1024]{2,1,0:T(4,128)S(1)}) custom-call(f32[2,16,128]{2,1,0:T(8,128)} %bitcast.12, f32[2,16,128]{2,1,0:T(8,128)} %bitcast.13, f32[4,16,128]{2,1,0:T(8,128)} %bitcast.10, f32[4,16,128]{2,1,0:T(8,128)} %bitcast.11, s32[1,16]{1,0:T(1,128)} %fill_hbm.1, f32[2,4,1024]{2,1,0:T(4,128)} %force_hbm.1, ...), custom_call_target="tpu_custom_call" | custom-call | tf_op jit(solution)/shard_map/pallas_call | solution.py:756
  44.8 0.6 %copy.12 = f32[12,1,16,128]{3,2,1,0:T(8,128)} copy(f32[12,1,16,128]{3,2,1,0:T(8,128)S(1)} %bitcast.8) | data formatting | bytes 196608
  45.4 0.6 %copy.13 = f32[2,4,1024]{2,1,0:T(4,128)} copy(f32[2,4,1024]{2,1,0:T(4,128)S(1)} %get-tuple-element.11) | data formatting | bytes 65536

commit v5 on v4

--- a/solution.py
+++ b/solution.py
@@ -22,8 +22,6 @@
 EXCHANGES = 8
 MAX_CH = 5
 CHUNKS = 1
-SCATTER_BLOCKS = (tuple(range(NB)),)
-GATHER_BLOCKS = (tuple(range(NB)),)
 CHUNK_COLS = (tuple(range(COLS)),)
 OWN = STEPS
 RAW, STRAIN, COT, FORCE, RATES, ADJ, FGRAD = range(7)
@@ -111,6 +109,7 @@
     st,
     amat,
     hot,
+    toh,
     qm,
     ev,
     od,
@@ -317,34 +316,54 @@
                 qm[21 + 3 * a + j] = w[j] * x[2 * a]
         qm[30] = st[k, 0]
 
-    def scatter(k, rows, blocks=range(NB)):
-        for b in blocks:
-            d = rows8 - jnp.broadcast_to(qm[30, pl.ds(b, 1), :], (8, 128))
-            nr, _, _ = row_spline(d)
-            nd = nr * d
-            pieces = []
-            for channel in rows:
-                for q, m in channel:
-                    x = nr * jnp.broadcast_to(qm[q, pl.ds(b, 1), :], (8, 128))
-                    if m is not None:
-                        x = x + nd * jnp.broadcast_to(qm[m, pl.ds(b, 1), :], (8, 128))
-                    pieces.append(split_rows(x))
-            lhs = jnp.concatenate(pieces, axis=0).astype(BF16)
+    def turn_hot(k):
+        for b in range(NB):
+            toh[k, b] = hot[k, b].T
+
+    def pair_hot(ref, k, i, zero):
+        return jnp.concatenate(
+            [
+                jnp.concatenate([ref[k, 2 * i], zero], axis=1),
+                jnp.concatenate([zero, ref[k, 2 * i + 1]], axis=1),
+            ],
+            axis=0,
+        )
+
+    def scatter(k, rows, turned=False):
+        zero = jnp.zeros((128, NP), BF16)
+        for i in range(NB // 2):
+            sides = []
+            for b in (2 * i, 2 * i + 1):
+                d = rows8 - jnp.broadcast_to(qm[30, pl.ds(b, 1), :], (8, 128))
+                nr, _, _ = row_spline(d)
+                nd = nr * d
+                pieces = []
+                for channel in rows:
+                    for q, m in channel:
+                        x = nr * jnp.broadcast_to(qm[q, pl.ds(b, 1), :], (8, 128))
+                        if m is not None:
+                            x = x + nd * jnp.broadcast_to(qm[m, pl.ds(b, 1), :], (8, 128))
+                        pieces.append(split_rows(x))
+                sides.append(jnp.concatenate(pieces, axis=0).astype(BF16))
             out = lax.dot_general(
-                lhs, hot[k, b], (((1,), (1,)), ((), ())), preferred_element_type=F32
+                jnp.concatenate(sides, axis=1),
+                pair_hot(toh if turned else hot, k, i, zero),
+                (((1,), (0 if turned else 1,)), ((), ())),
+                preferred_element_type=F32,
             )
-            target = ev if b % 2 == 0 else od
-            for ch in range(len(rows)):
-                total = None
-                for j, s in enumerate(SHIFTS):
-                    at = (3 * ch + j) * 16
-                    value = out[at : at + 8] + out[at + 8 : at + 16]
-                    if s:
-                        value = roll(value, s)
-                    total = value if total is None else total + value
-                if b % 2:
-                    total = roll(total, 64)
-                target[ch, b // 2] = total
+            for side, target in enumerate((ev, od)):
+                for ch in range(len(rows)):
+                    total = None
+                    for j, s in enumerate(SHIFTS):
+                        at = (3 * ch + j) * 16
+                        value = out[at : at + 16, 128 * side : 128 * side + 128]
+                        value = value[:8] + value[8:]
+                        if s:
+                            value = roll(value, s)
+                        total = value if total is None else total + value
+                    if side:
+                        total = roll(total, 64)
+                    target[ch, i] = total
 
     def forward_channels():
         return [[(j, None) for j in range(3)]] + [
@@ -396,7 +415,7 @@
 
     def scatter_and_send(e, k, rows, part, force_role, targets, before_first=None):
         for c in range(CHUNKS):
-            scatter(k, rows, SCATTER_BLOCKS[c])
+            scatter(k, rows, len(rows) == 2)
             combine(len(rows), part, force_role, CHUNK_COLS[c])
             pack(e, c, len(rows), part)
             if before_first is not None and c == 0:
@@ -438,22 +457,26 @@
                     part[1 + a, :, at] = value
                     fgacc[a, :, at] = DT * value if initial else fgacc[a, :, at] + DT * value
 
-    def gather(k, column, channels, blocks):
+    def gather(k, column, channels):
         stride = 3 * channels * 64
-        for b in blocks:
-            i = b // 2
-            pieces = []
+        zero = jnp.zeros((128, NP), BF16)
+        for i in range(NB // 2):
+            pieces = ([], [])
             for ch in range(channels):
                 window = column(ch, i)
-                if b % 2:
-                    window = roll(jnp.where(left_half, column(ch, (i + 1) % COLS), window), 64)
+                shifted = roll(jnp.where(left_half, column(ch, (i + 1) % COLS), window), 64)
                 for s in SHIFTS:
-                    pieces.append(split_rows(roll(window, -s) if s else window))
-            lhs = jnp.concatenate(pieces, axis=0).astype(BF16)
-            out = jnp.dot(lhs, hot[k, b], preferred_element_type=F32)
-            for q in range(3 * channels):
-                value = out[16 * q : 16 * q + 8] + out[16 * q + 8 : 16 * q + 16]
-                gat[pl.ds((b // 8) * stride + q * 64 + b % 8, 8, stride=8), :] = value
+                    pieces[0].append(split_rows(roll(window, -s) if s else window))
+                    pieces[1].append(split_rows(roll(shifted, -s) if s else shifted))
+            lhs = jnp.concatenate(
+                [jnp.concatenate(side, axis=0).astype(BF16) for side in pieces], axis=1
+            )
+            out = jnp.dot(lhs, pair_hot(hot, k, i, zero), preferred_element_type=F32)
+            for side in range(2):
+                b = 2 * i + side
+                for q in range(3 * channels):
+                    rows = out[16 * q : 16 * q + 16, 128 * side : 128 * side + 128]
+                    gat[pl.ds((b // 8) * stride + q * 64 + b % 8, 8, stride=8), :] = rows[:8] + rows[8:]
 
     def gathered(half, channels, q, r):
         return gat[pl.ds(half * 3 * channels * 64 + q * 64 + r * 8, 8), :]
@@ -616,14 +639,14 @@
         for c in range(CHUNKS):
             wait_halo(e, c, 3, targets)
             grid_velocity(k, e, c, part)
-            gather(k, grid_column(k), 2, GATHER_BLOCKS[c])
+            gather(k, grid_column(k), 2)
         advance(k, True)
 
     def backward_back(k, e, part, initial, targets):
         for c in range(CHUNKS):
             wait_halo(e, c, 2, targets)
             grid_adjoint(k, e, c, 0, part, initial)
-            gather(k, part_column(part), 3, GATHER_BLOCKS[c])
+            gather(k, part_column(part), 3)
 
     part, part_own = parts.at[0], parts.at[1]
     adj, adj_own = adjs.at[0], adjs.at[1]
@@ -639,7 +662,8 @@
         barrier_wait()
         start_move(RAW)
 
-    scatter_and_send(0, OWN, forward_channels(), part_own, 1, to_hosts, enter)
+    enter()
+    scatter_and_send(0, OWN, forward_channels(), part_own, 1, to_hosts)
     start_move(FORCE)
     start_move(STRAIN)
     start_move(COT)
@@ -662,7 +686,9 @@
         forward_front(k, 0)
         scatter_and_send(k, k, forward_channels(), part, 0, ring)
         save_slopes(k - 1)
+        turn_hot(k - 1)
         if k == 1:
+            turn_hot(OWN)
             for c in range(CHUNKS):
                 wait_halo(7, c, 3, owners, 0)
                 grid_velocity(OWN, 7, c, part_own)
@@ -677,6 +703,7 @@
     build_hot(last)
     scatter_and_send(last, last, forward_channels() + adjoint_channels(15), part, 0, ring)
     save_slopes(last - 1)
+    turn_hot(last - 1)
 
     def last_column(ch, i):
         return grid_column(last)(ch, i) if ch < 2 else part_column(part)(ch - 2, i)
@@ -685,7 +712,7 @@
         wait_halo(last, c, 5, ring)
         grid_velocity(last, last, c, part)
         grid_adjoint(last, last, c, 3, part, True)
-        gather(last, last_column, 5, GATHER_BLOCKS[c])
+        gather(last, last_column, 5)
     advance(last, False, 5)
     save_slopes(last, 5)
     v, x = adjoint_rows(last, 15, adj)
@@ -707,7 +734,8 @@
     v, x = adjoint_rows(0, 15, adj)
     for i, value in enumerate(v + x):
         rates[0, i] = value
-    scatter_and_send(6, 0, adjoint_channels(15), part, None, to_owners, lambda: start_move(RATES))
+    start_move(RATES)
+    scatter_and_send(6, 0, adjoint_channels(15), part, None, to_owners)
     pull_gather(0, v, x, adj)
     for i in range(6):
         rest[0, i] = adj[i if i < 2 else 6 + i]
@@ -718,7 +746,7 @@
 
     end_move(RATES, rates, 0, 1)
     rate_rows(OWN)
-    scatter(OWN, adjoint_channels(15))
+    scatter(OWN, adjoint_channels(15), True)
     combine(2, part_own, None)
     backward_back(OWN, 6, part_own, True, to_owners)
     end_move(ADJ, rest, 0, 1)
@@ -774,6 +802,7 @@
             pltpu.VMEM((STEPS + 1, 12, NB, NP), F32),
             pltpu.VMEM((STEPS + 1, 4, NB, NP), F32),
             pltpu.VMEM((STEPS + 1, NB, 128, NP), BF16),
+            pltpu.VMEM((STEPS + 1, NB, NP, 128), BF16),
             pltpu.VMEM((32, NB, NP), F32),
             pltpu.VMEM((MAX_CH, COLS, 8, 128), F32),
             pltpu.VMEM((MAX_CH, COLS, 8, 128), F32),

time: 46.4 us -> 44.5 us (0.959)
  Pallas kernels: 44.1 us -> 42.4 us
    pallas_call x1, Pallas kernels: 44.1 us -> 42.4 us  [per_device(): pl.pallas_call(functools.partial(kernel, n), out_shape=(jax.ShapeDtypeStr...]
where the time goes in v5:
time: 44.5 us; the launch traced here: 44.3 us
  Pallas kernels  42.4 us (95%)
  local copies, waits for them, and re-layouts  1.26 us (3%)
  between operations  0.64 us (1%)
    pallas_call x1, Pallas kernels, per_device(): pl.pallas_call(functools.partial(kernel, n), out_shape=(jax.ShapeDtypeStr...  42.4 us
    unnamed x2, local copies, waits for them, and re-layouts  1.26 us

profile of v5, /device:TPU:0, one launch (start us, length us, event | category | flops | bytes accessed | tf_op | source)
XLA Modules:
  0.0 44.3 jit_solution(11960196373859285125)
XLA Ops:
  0.6 42.4 %shard_map.86 = (f32[12,16,128]{2,1,0:T(8,128)S(1)}, f32[2,4,1024]{2,1,0:T(4,128)S(1)}) custom-call(f32[2,16,128]{2,1,0:T(8,128)} %bitcast.12, f32[2,16,128]{2,1,0:T(8,128)} %bitcast.13, f32[4,16,128]{2,1,0:T(8,128)} %bitcast.10, f32[4,16,128]{2,1,0:T(8,128)} %bitcast.11, s32[1,16]{1,0:T(1,128)} %fill_hbm.1, f32[2,4,1024]{2,1,0:T(4,128)} %force_hbm.1, ...), custom_call_target="tpu_custom_call" | custom-call | tf_op jit(solution)/shard_map/pallas_call | solution.py:784
  43.0 0.6 %copy.12 = f32[12,1,16,128]{3,2,1,0:T(8,128)} copy(f32[12,1,16,128]{3,2,1,0:T(8,128)S(1)} %bitcast.8) | data formatting | bytes 196608
  43.7 0.6 %copy.13 = f32[2,4,1024]{2,1,0:T(4,128)} copy(f32[2,4,1024]{2,1,0:T(4,128)S(1)} %get-tuple-element.11) | data formatting | bytes 65536

commit v6 on v5

--- a/solution.py
+++ b/solution.py
@@ -666,28 +666,35 @@
     scatter_and_send(0, OWN, forward_channels(), part_own, 1, to_hosts)
     start_move(FORCE)
     start_move(STRAIN)
-    start_move(COT)
-    for c in range(CHUNKS):
-        start_halo(7, c, 3, owners, 0)
 
     end_move(RAW, first, 1, 0)
     host_state()
     forward_front(0, 0)
     scatter(0, forward_channels())
+    combine(3, part, None)
+    for c in range(CHUNKS):
+        wait_halo(0, c, 3, to_hosts)
     end_move(FORCE, force, 1, 0)
     place_force(0)
-    combine(3, part, 0)
+    for a in range(2):
+        part[1 + a] = part[1 + a] + frc[0, a]
+    for c in range(CHUNKS):
+        grid_velocity(0, 0, c, part)
+        gather(0, grid_column(0), 2)
     end_move(STRAIN, strn, 1, 0)
     for i in range(4):
         st[0, 8 + i] = strn[0, i] + (1.0 if i in (0, 3) else 0.0)
-    forward_back(0, 0, part, to_hosts)
+    advance(0, True)
+    start_move(COT)
+    for c in range(CHUNKS):
+        start_halo(7, c, 3, owners, 0)
 
     for k in range(1, last):
         forward_front(k, 0)
         scatter_and_send(k, k, forward_channels(), part, 0, ring)
         save_slopes(k - 1)
         turn_hot(k - 1)
-        if k == 1:
+        if k == 2:
             turn_hot(OWN)
             for c in range(CHUNKS):
                 wait_halo(7, c, 3, owners, 0)

time: 44.5 us -> 44.6 us (level)
  no operation moved by 1% of the time
where the time goes in v6:
time: 44.6 us; the launch traced here: 44.5 us
  Pallas kernels  42.6 us (96%)
  local copies, waits for them, and re-layouts  1.26 us (3%)
  between operations  0.64 us (1%)
    pallas_call x1, Pallas kernels, per_device(): pl.pallas_call(functools.partial(kernel, n), out_shape=(jax.ShapeDtypeStr...  42.6 us
    unnamed x2, local copies, waits for them, and re-layouts  1.26 us

profile of v6, /device:TPU:0, one launch (start us, length us, event | category | flops | bytes accessed | tf_op | source)
XLA Modules:
  0.0 44.5 jit_solution(10945425366304979440)
XLA Ops:
  0.6 42.6 %shard_map.86 = (f32[12,16,128]{2,1,0:T(8,128)S(1)}, f32[2,4,1024]{2,1,0:T(4,128)S(1)}) custom-call(f32[2,16,128]{2,1,0:T(8,128)} %bitcast.12, f32[2,16,128]{2,1,0:T(8,128)} %bitcast.13, f32[4,16,128]{2,1,0:T(8,128)} %bitcast.10, f32[4,16,128]{2,1,0:T(8,128)} %bitcast.11, s32[1,16]{1,0:T(1,128)} %fill_hbm.1, f32[2,4,1024]{2,1,0:T(4,128)} %force_hbm.1, ...), custom_call_target="tpu_custom_call" | custom-call | tf_op jit(solution)/shard_map/pallas_call | solution.py:791
  43.2 0.6 %copy.12 = f32[12,1,16,128]{3,2,1,0:T(8,128)} copy(f32[12,1,16,128]{3,2,1,0:T(8,128)S(1)} %bitcast.8) | data formatting | bytes 196608
  43.9 0.6 %copy.13 = f32[2,4,1024]{2,1,0:T(4,128)} copy(f32[2,4,1024]{2,1,0:T(4,128)S(1)} %get-tuple-element.11) | data formatting | bytes 65536
